TPU v7x, 64 devices: a 2x2x8 block of a 4x4x8 slice. The times are simulated.
64 devices in a mesh: dp: 4 (over x, y), tp: 16 (over z, core).
Axes of the slice: x: 2, y: 2, z: 8, core: 2. Of those that a mesh axis runs over, the one named last changes fastest.
The devices are a block of a 4x4x8 slice.
Arguments:
- hidden: bfloat16 [2048, 7168], P(('dp', 'tp')), parts along dimension 0
- cache_lat: bfloat16 [2048, 128, 512], P(('dp', 'tp')), parts along dimension 0
- cache_rope: bfloat16 [2048, 128, 64], P(('dp', 'tp')), parts along dimension 0
- seq_lens: int32 [2048], P(('dp', 'tp')), parts along dimension 0
- attn_norm: bfloat16 [7168], replicated
- w_query: bfloat16 [7168, 12288], replicated
- w_kv_down: bfloat16 [7168, 576], replicated
- kv_norm: bfloat16 [512], replicated
- w_key_up: bfloat16 [512, 8192], replicated
- w_val_up: bfloat16 [512, 8192], replicated
- w_out: bfloat16 [8192, 7168], replicated
- mlp_norm: bfloat16 [7168], replicated
- w_gate: bfloat16 [7168, 18432], P(None, 'tp')
- w_up: bfloat16 [7168, 18432], P(None, 'tp')
- w_down: bfloat16 [18432, 7168], P('tp')
Outputs:
- output 1: bfloat16 [2048, 7168], P(('dp', 'tp')), parts along dimension 0
- output 2: bfloat16 [2048, 512], P(('dp', 'tp')), parts along dimension 0
- output 3: bfloat16 [2048, 64], P(('dp', 'tp')), parts along dimension 0
There are 4 independent parts. A program takes and returns all parts, laid end to end along the dimension named above; an argument that names none is the same for every part.
All inputs are finite; a program needn't handle non-finite values.
Results may differ from a plain program's by a relative error of at most 0.0117004.
Values are sent between devices in bfloat16 or wider.
A program may use at most 768 MiB of HBM per device.

v0:
```python
import jax
import jax.numpy as jnp
from jax import lax
from jax.sharding import PartitionSpec as P

EPS = 1e-6
ROPE_BASE = 10000.0
value_a7 = 512
ROPE_DIM = 64
NOPE_DIM = 128
SCALE = (NOPE_DIM + ROPE_DIM) ** -0.5


def rms_norm(vals, gain):
    vals32 = vals.astype(jnp.float32)
    inv_rms = lax.rsqrt(jnp.mean(vals32 * vals32, axis=-1, keepdims=True) + EPS)
    return (vals32 * inv_rms * gain.astype(jnp.float32)).astype(jnp.bfloat16)


def rotate(vals, cos_tab, sin_tab):
    half = vals.shape[-1] // 2
    first = vals[..., :half]
    second = vals[..., half:]
    return jnp.concatenate([first * cos_tab - second * sin_tab, second * cos_tab + first * sin_tab], axis=-1)


def rope_tables(seq_lens):
    inv_freq = ROPE_BASE ** (-jnp.arange(0, ROPE_DIM, 2, dtype=jnp.float32) / ROPE_DIM)
    angles = seq_lens.astype(jnp.float32)[:, None] * inv_freq[None, :]
    return jnp.cos(angles), jnp.sin(angles)


def attention_block(hidden, cache_lat, cache_rope, seq_lens, attn_norm, w_query, w_kv_down, kv_norm, w_key_up, w_val_up, w_out):
    rows = hidden.shape[0]
    heads = w_key_up.shape[1] // NOPE_DIM
    normed = rms_norm(hidden, attn_norm)
    query = jnp.dot(normed, w_query, preferred_element_type=jnp.float32).astype(jnp.bfloat16).reshape(rows, heads, NOPE_DIM + ROPE_DIM)
    kv_proj = jnp.dot(normed, w_kv_down, preferred_element_type=jnp.float32).astype(jnp.bfloat16)
    lat_new = rms_norm(kv_proj[:, :value_a7], kv_norm)
    cos_tab, sin_tab = rope_tables(seq_lens)
    rope_new = rotate(kv_proj[:, value_a7:].astype(jnp.float32), cos_tab, sin_tab).astype(jnp.bfloat16)
    q_rot = rotate(query[:, :, NOPE_DIM:].astype(jnp.float32), cos_tab[:, None, :], sin_tab[:, None, :]).astype(jnp.bfloat16)
    key_up = w_key_up.reshape(value_a7, heads, NOPE_DIM)
    q_lat = jnp.einsum('bhn,khn->bhk', query[:, :, :NOPE_DIM], key_up, preferred_element_type=jnp.float32).astype(jnp.bfloat16)
    scores = (jnp.einsum('bhk,bsk->bhs', q_lat, cache_lat, preferred_element_type=jnp.float32) + jnp.einsum('bhr,bsr->bhs', q_rot, cache_rope, preferred_element_type=jnp.float32)) * SCALE
    score_new = (jnp.einsum('bhk,bk->bh', q_lat, lat_new, preferred_element_type=jnp.float32) + jnp.einsum('bhr,br->bh', q_rot, rope_new, preferred_element_type=jnp.float32)) * SCALE
    slots = cache_lat.shape[1]
    valid = jnp.arange(slots)[None, None, :] < seq_lens[:, None, None]
    scores = jnp.where(valid, scores, -jnp.inf)
    top = jnp.maximum(jnp.max(scores, axis=-1), score_new)
    expo = jnp.exp(scores - top[..., None])
    expo_new = jnp.exp(score_new - top)
    denom = jnp.sum(expo, axis=-1) + expo_new
    probs = (expo / denom[..., None]).astype(jnp.bfloat16)
    prob_new = (expo_new / denom).astype(jnp.bfloat16)
    lat_sum = jnp.einsum('bhs,bsk->bhk', probs, cache_lat, preferred_element_type=jnp.float32) + prob_new.astype(jnp.float32)[..., None] * lat_new.astype(jnp.float32)[:, None, :]
    lat_out = lat_sum.astype(jnp.bfloat16)
    val_up = w_val_up.reshape(value_a7, heads, -1)
    head_out = jnp.einsum('bhk,khv->bhv', lat_out, val_up, preferred_element_type=jnp.float32).astype(jnp.bfloat16).reshape(rows, -1)
    attn_out = jnp.dot(head_out, w_out, preferred_element_type=jnp.float32)
    resid = (hidden.astype(jnp.float32) + attn_out).astype(jnp.bfloat16)
    return resid, lat_new, rope_new


def solution(mesh):
    rows_spec = P(('dp', 'tp'), None)
    cache_spec = P(('dp', 'tp'), None, None)
    whole = P()
    in_specs = (rows_spec, cache_spec, cache_spec, P(('dp', 'tp')), whole, whole, whole, whole, whole, whole, whole, whole, P(None, 'tp'), P(None, 'tp'), P('tp', None))
    out_specs = (rows_spec, rows_spec, rows_spec)

    def device_step(hidden, cache_lat, cache_rope, seq_lens, attn_norm, w_query, w_kv_down, kv_norm, w_key_up, w_val_up, w_out, mlp_norm, w_gate, w_up, w_down):
        resid, lat_new, rope_new = attention_block(hidden, cache_lat, cache_rope, seq_lens, attn_norm, w_query, w_kv_down, kv_norm, w_key_up, w_val_up, w_out)
        mlp_in = rms_norm(resid, mlp_norm)
        group_in = lax.all_gather(mlp_in, 'tp', axis=0, tiled=True)
        gate_proj = jnp.dot(group_in, w_gate, preferred_element_type=jnp.float32)
        up_proj = jnp.dot(group_in, w_up, preferred_element_type=jnp.float32)
        act = (jax.nn.silu(gate_proj) * up_proj).astype(jnp.bfloat16)
        partial_out = jnp.dot(act, w_down, preferred_element_type=jnp.float32).astype(jnp.bfloat16)
        mlp_out = lax.psum_scatter(partial_out, 'tp', scatter_dimension=0, tiled=True)
        out_hidden = (resid.astype(jnp.float32) + mlp_out.astype(jnp.float32)).astype(jnp.bfloat16)
        return out_hidden, lat_new, rope_new

    return jax.shard_map(device_step, mesh=mesh, in_specs=in_specs, out_specs=out_specs, check_vma=False)
```

profile of v0, /device:TPU:21, one launch (start us, length us, event | category | flops | bytes accessed | tf_op | source)
XLA Modules:
  0.0 304.7 jit_solution(7070411528453335075)
XLA Ops:
  7.3 0.8 convert_element_type.95
  8.0 0.7 iota_compare_fusion
  8.8 1.2 fusion.39
  10.0 0.7 convert_element_type.89
  10.7 6.0 %convolution_convert_fusion.2 = bf16[32,576]{1,0:T(8,128)(2,1)S(1)} fusion(bf16[7168,576]{0,1:T(8,128)(2,1)} %param.21, bf16[32,7168]{1,0:T(8,128)(2,1)} %param.15, f32[7168]{0:T(1024)S(1)} %convert_element_type.89, f32[32]{0:T(128)S(1)} %add_rsqrt_fusion.2), kind=kOutput, calls=%fused_computation.29 | convolution fusion | flops 265177088 | bytes 8781952 | tf_op jit(solution)/shard_map/dot_general | solution.py:38
  16.9 56.7 %convolution_convert_fusion = bf16[32,12288]{1,0:T(8,128)(2,1)S(1)} fusion(bf16[7168,12288]{1,0:T(8,128)(2,1)} %param.20, bf16[32,7168]{1,0:T(8,128)(2,1)S(1)} %copy-done.3, f32[7168]{0:T(1024)S(1)} %convert_element_type.89, f32[32]{0:T(128)S(1)} %add_rsqrt_fusion.2), kind=kOutput, calls=%fused_computation | convolution fusion | flops 5638455296 | bytes 177434752 | tf_op jit(solution)/shard_map/dot_general | solution.py:37
  73.5 1.2 reshape.122
  75.2 0.6 subtract_convert_fusion
  75.8 0.4 fusion.50
  76.8 6.5 %convert_bitcast_fusion = bf16[32,64,512]{2,0,1:T(8,128)(2,1)S(1)} fusion(bf16[32,64,128]{2,1,0:T(8,128)(2,1)S(1)} %slice.32, bf16[512,8192]{1,0:T(8,128)(2,1)} %param.23), kind=kOutput, calls=%fused_computation.17 | convolution fusion | flops 269484032 | bytes 11010048 | tf_op jit(solution)/shard_map/bhn,khn->bhk/dot_general | solution.py:44
  83.3 1.2 fusion.15
  84.6 2.8 fusion.64
  87.3 0.7 fusion.38
  88.1 3.0 fusion.42
  91.1 7.0 %fusion.33 = bf16[64,4,8,128]{3,2,1,0:T(8,128)(2,1)S(1)} fusion(f32[32,64,512]{2,1,0:T(8,128)S(1)} %fusion.42, f32[32,512]{1,0:T(8,128)S(1)} %get-tuple-element.3, f32[32,64]{0,1:T(8,128)S(1)} %copy.26, bf16[512,8192]{1,0:T(8,128)(2,1)} %param.24), kind=kOutput, calls=%fused_computation.28 | convolution fusion | flops 271843328 | bytes 13180928 | tf_op jit(solution)/shard_map/bhk,khv->bhv/dot_general | solution.py:59
  98.2 39.7 %multiply_reduce_fusion = (f32[32]{0:T(128)S(1)}, f32[32,7168]{1,0:T(8,128)S(1)}) fusion(bf16[8192,7168]{1,0:T(8,128)(2,1)} %param.25, bf16[64,4,8,128]{3,2,1,0:T(8,128)(2,1)S(1)} %fusion.33, bf16[32,7168]{1,0:T(8,128)(2,1)S(1)} %copy-done.3), kind=kOutput, calls=%fused_computation.40 | convolution fusion | flops 3759472640 | bytes 119341184 | tf_op jit(solution)/shard_map/dot_general | solution.py:60
  137.9 0.9 multiply_convert_fusion
  138.9 52.7 %all-gather.2.cloned.1.call-done = bf16[512,7168]{1,0:T(8,128)(2,1)} async-done(((bf16[32,7168]{1,0:T(8,128)(2,1)}), bf16[512,7168]{1,0:T(8,128)(2,1)}) %all-gather.2.cloned.1.call-update) | async-done | bytes 7340048 | tf_op jit(solution)/shard_map/all_gather | solution.py:75
  191.6 15.9 %fusion.65 = f32[512,1152]{1,0:T(8,128)} fusion(bf16[512,7168]{1,0:T(8,128)(2,1)} %all-gather.2.cloned.1.call-done, bf16[7168,1152]{1,0:T(8,128)(2,1)} %param.27), kind=kOutput, calls=%fused_computation.79 | convolution fusion | flops 8455716864 | bytes 26214400 | tf_op jit(solution)/shard_map/dot_general | solution.py:76
  207.5 15.7 %fusion.9 = bf16[512,1152]{1,0:T(8,128)(2,1)S(1)} fusion(bf16[512,7168]{1,0:T(8,128)(2,1)} %all-gather.2.cloned.1.call-done, bf16[7168,1152]{1,0:T(8,128)(2,1)} %param.28, f32[512,1152]{1,0:T(8,128)} %fusion.65), kind=kOutput, calls=%fused_computation.14 | convolution fusion | flops 8459255808 | bytes 27394048 | tf_op jit(solution)/shard_map/dot_general | solution.py:77
  223.3 11.7 %convolution_convert_fusion.1 = bf16[512,7168]{1,0:T(8,128)(2,1)} fusion(bf16[512,1152]{1,0:T(8,128)(2,1)S(1)} %fusion.9, bf16[1152,7168]{1,0:T(8,128)(2,1)S(1)} %bitcast.56), kind=kOutput, calls=%fused_computation.1 | convolution fusion | flops 8459386880 | bytes 25034752 | tf_op jit(solution)/shard_map/dot_general | solution.py:79
  235.0 0.7 pad_maximum_fusion.3
  235.7 60.3 %reduce-scatter.2.cloned.1.call-done = bf16[32,7168]{1,0:T(8,128)(2,1)} async-done(((bf16[512,7168]{1,0:T(8,128)(2,1)}), bf16[32,7168]{1,0:T(8,128)(2,1)}) %reduce-scatter.2.cloned.1.call-update) | async-done | bytes 458768 | tf_op jit(solution)/shard_map/reduce_scatter | solution.py:80
  296.0 1.9 add_convert_fusion.1
  (44 shorter events, 1.5 us)
Async XLA Ops:
  7.2 69.1 %copy-start = (bf16[32,128,64]{1,2,0:T(8,128)(2,1)S(1)}, bf16[32,128,64]{1,2,0:T(8,128)(2,1)}, u32[]{:S(2)}) copy-start(bf16[32,128,64]{1,2,0:T(8,128)(2,1)} %param.17) | copy-start | bytes 1572868
  7.2 9.6 %copy-start.3 = (bf16[32,7168]{1,0:T(8,128)(2,1)S(1)}, bf16[32,7168]{1,0:T(8,128)(2,1)}, u32[]{:S(2)}) copy-start(bf16[32,7168]{1,0:T(8,128)(2,1)} %param.15) | copy-start | bytes 1376260
  7.2 184.4 %all-gather.2.cloned.1.call-start = ((), (), s32[]{:S(2)}) async-start(), calls=%async_computation.1 | async-start | bytes 7798784 | tf_op jit(solution)/shard_map/all_gather | solution.py:75
  16.8 58.1 %copy-start.6 = (bf16[512]{0:T(512)(128)(2,1)S(1)}, bf16[512]{0:T(512)(128)(2,1)}, u32[]{:S(2)}) copy-start(bf16[512]{0:T(512)(128)(2,1)} %param.22) | copy-start | bytes 3076
  16.9 58.1 %copy-start.5 = (bf16[7168]{0:T(1024)(128)(2,1)S(1)}, bf16[7168]{0:T(1024)(128)(2,1)}, u32[]{:S(2)}) copy-start(bf16[7168]{0:T(1024)(128)(2,1)} %param.26) | copy-start | bytes 43012
  76.7 7.9 %copy-start.2 = (bf16[32,128,512]{2,1,0:T(8,128)(2,1)S(1)}, bf16[32,128,512]{2,1,0:T(8,128)(2,1)}, u32[]{:S(2)}) copy-start(bf16[32,128,512]{2,1,0:T(8,128)(2,1)} %param.16) | copy-start | bytes 12582916
  76.8 10.5 %copy-start.4 = (bf16[32,512]{1,0:T(8,128)(2,1)}, bf16[32,512]{1,0:T(8,128)(2,1)S(1)}, u32[]{:S(2)}) copy-start(bf16[32,512]{1,0:T(8,128)(2,1)S(1)} %get-tuple-element.4) | copy-start | bytes 98308
  138.9 157.1 %reduce-scatter.2.cloned.1.call-start = ((), (), s32[]{:S(2)}) async-start(), calls=%async_computation.2 | async-start | bytes 7798784 | tf_op jit(solution)/shard_map/reduce_scatter | solution.py:80
  191.6 31.6 %slice-start = ((s8[16515072]{0:T(1024)(128)(4,1)}), s8[4194304]{0:T(1024)(128)(4,1)S(1)}, s32[]{:S(2)}) async-start(s8[16515072]{0:T(1024)(128)(4,1)} %bitcast.55), calls=%async_computation.3 | async-start | bytes 8388608
  191.6 31.6 %slice-start.1 = ((s8[16515072]{0:T(1024)(128)(4,1)}), s8[4194304]{0:T(1024)(128)(4,1)S(1)}, s32[]{:S(2)}) async-start(s8[16515072]{0:T(1024)(128)(4,1)} %bitcast.55), calls=%async_computation.4 | async-start | bytes 8388608
  207.5 15.7 %slice-start.2 = ((s8[16515072]{0:T(1024)(128)(4,1)}), s8[4194304]{0:T(1024)(128)(4,1)S(1)}, s32[]{:S(2)}) async-start(s8[16515072]{0:T(1024)(128)(4,1)} %bitcast.55), calls=%async_computation.5 | async-start | bytes 8388608
  207.5 15.7 %slice-start.3 = ((s8[16515072]{0:T(1024)(128)(4,1)}), s8[3932160]{0:T(1024)(128)(4,1)S(1)}, s32[]{:S(2)}) async-start(s8[16515072]{0:T(1024)(128)(4,1)} %bitcast.55), calls=%async_computation.6 | async-start | bytes 7864320
  223.3 74.6 %copy-start.1 = (bf16[32,128,64]{1,2,0:T(8,128)(2,1)S(1)}, bf16[32,128,64]{1,2,0:T(8,128)(2,1)}, u32[]{:S(2)}) copy-start(bf16[32,128,64]{1,2,0:T(8,128)(2,1)} %param.17) | copy-start | bytes 1572868
Sparse Core Ops, SparseCore 0:
  139.0 52.5 all-gather.1
  235.1 60.8 reduce-scatter.1
where the time goes:
time: 307 us; the launch traced here: 305 us
  matrix products  167 us (54%)
  waiting for transfers between devices  113 us (37%)
  between operations  14.3 us (5%)
  other arithmetic  8.74 us (3%)
    reduce_scatter x1, waiting for transfers between devices, device_step(): lax.psum_scatter(partial_out, 'tp', scatter_dimension=0, tiled=True)  60.3 us
    dot_general x1, matrix products, attention_block(): jnp.dot(normed, w_query, preferred_element_type=jnp.float32)  56.7 us
    all_gather x1, waiting for transfers between devices, device_step(): group_in = lax.all_gather(mlp_in, 'tp', axis=0, tiled=True)  52.7 us
    dot_general x1, matrix products, attention_block(): attn_out = jnp.dot(head_out, w_out, preferred_element_type=jnp.float32)  39.7 us
    dot_general x1, matrix products, device_step(): gate_proj = jnp.dot(group_in, w_gate, preferred_element_type=jnp.float32)  15.9 us
    dot_general x1, matrix products, device_step(): up_proj = jnp.dot(group_in, w_up, preferred_element_type=jnp.float32)  15.7 us
    dot_general x1, matrix products, device_step(): jnp.dot(act, w_down, preferred_element_type=jnp.float32)  11.7 us
    dot_general x1, matrix products, attention_block(): jnp.einsum('bhk,khv->bhv', lat_out, val_up, preferred_element_type=jnp.fl...  7.05 us
  transfers between devices with their start and end apart: 2, of which 2 were waited for; matrix products, arithmetic and copies ran while one was open for 0% of the time, Pallas kernels for 0%

commit v1 on v0

--- a/solution.py
+++ b/solution.py
@@ -1,6 +1,10 @@
+import functools
+
 import jax
 import jax.numpy as jnp
 from jax import lax
+from jax.experimental import pallas as pl
+from jax.experimental.pallas import tpu as pltpu
 from jax.sharding import PartitionSpec as P
 
 EPS = 1e-6
@@ -30,7 +34,7 @@
     return jnp.cos(angles), jnp.sin(angles)
 
 
-def attention_block(hidden, cache_lat, cache_rope, seq_lens, attn_norm, w_query, w_kv_down, kv_norm, w_key_up, w_val_up, w_out):
+def attention_block(hidden, cache_lat, cache_rope, seq_lens, attn_norm, w_query, w_kv_down, kv_norm, w_key_up, w_val_up):
     rows = hidden.shape[0]
     heads = w_key_up.shape[1] // NOPE_DIM
     normed = rms_norm(hidden, attn_norm)
@@ -57,9 +61,353 @@
     lat_out = lat_sum.astype(jnp.bfloat16)
     val_up = w_val_up.reshape(value_a7, heads, -1)
     head_out = jnp.einsum('bhk,khv->bhv', lat_out, val_up, preferred_element_type=jnp.float32).astype(jnp.bfloat16).reshape(rows, -1)
-    attn_out = jnp.dot(head_out, w_out, preferred_element_type=jnp.float32)
-    resid = (hidden.astype(jnp.float32) + attn_out).astype(jnp.bfloat16)
-    return resid, lat_new, rope_new
+    return head_out, lat_new, rope_new
+
+MESH = pl.DeviceIdType.MESH
+GATHER_LAG = 1
+SCATTER_LAG = 1
+
+
+def tail_kernel(n, tile, sub, o_ref, x_ref, gain_ref, wo_hbm, wg_hbm, wu_hbm, wd_hbm, out_ref,
+                o_all, x_half, gain_s, wo_buf, wgu_buf, x1_all, xg, acc, ssq, act_all, wd_all, part,
+                stage_up, stage_dn, ring_up, ring_dn, stage_out,
+                pre_send, pre_recv, wo_sem, wgu_sem, wd_sem, wdp_send, wdp_recv,
+                g_send, g_recv, p_send, p_recv, a_send, a_recv, r_send, r_recv, f_send, f_recv):
+    f32, bf16 = jnp.float32, jnp.bfloat16
+    rows, width = x_ref.shape
+    half = width // 2
+    tiles = half // tile
+    subs = tile // sub
+    ffn = wg_hbm.shape[1]
+    chips = n // 2
+    reach_max = chips // 2
+    chip_rows = 2 * rows
+    depth = part.shape[0]
+
+    me = lax.axis_index('tp')
+    core = lax.rem(me, 2)
+    chip = lax.div(me, 2)
+    other = 1 - core
+    partner = me + 1 - 2 * core
+    upper = lax.rem(me + 2, n)
+    lower = lax.rem(me + n - 2, n)
+    mine = pl.multiple_of(core * half, 128)
+    theirs = pl.multiple_of(other * half, 128)
+
+    def remote(src, dst, send_sem, recv_sem, dev):
+        return pltpu.make_async_remote_copy(src_ref=src, dst_ref=dst, send_sem=send_sem, recv_sem=recv_sem, device_id={'tp': dev}, device_id_type=MESH)
+
+    def wo_copy(i):
+        slot = lax.rem(i, 2)
+        return pltpu.make_async_copy(wo_hbm.at[:, pl.ds(pl.multiple_of(mine + i * sub, 128), sub)], wo_buf.at[slot], wo_sem.at[slot])
+
+    def wgu_copies(t):
+        slot = lax.rem(t, 2)
+        out = []
+        for h in range(2):
+            for k, src in enumerate((wg_hbm, wu_hbm)):
+                out.append(pltpu.make_async_copy(src.at[pl.ds(pl.multiple_of(h * half + t * tile, 128), tile), :], wgu_buf.at[slot, pl.ds(h * tile, tile), pl.ds(k * ffn, ffn)], wgu_sem.at[slot, 2 * h + k]))
+        return out
+
+    def wd_copy(t):
+        return pltpu.make_async_copy(wd_hbm.at[:, pl.ds(pl.multiple_of(mine + t * tile, 128), tile)], wd_all.at[t, pl.ds(pl.multiple_of(core * ffn, 128), ffn), :], wd_sem.at[t])
+
+    def wd_push(t):
+        return remote(wd_hbm.at[:, pl.ds(pl.multiple_of(theirs + t * tile, 128), tile)], wd_all.at[t, pl.ds(pl.multiple_of(core * ffn, 128), ffn), :], wdp_send.at[t], wdp_recv.at[t], partner)
+
+    def wd_arrival(t):
+        return remote(wd_hbm.at[:, pl.ds(0, tile)], wd_all.at[t, pl.ds(pl.multiple_of(other * ffn, 128), ffn), :], wdp_send.at[t], wdp_recv.at[t], partner)
+
+    wo_copy(0).start()
+    wo_copy(1).start()
+
+    barrier = pltpu.get_barrier_semaphore()
+    for dev in (partner, upper, lower):
+        pl.semaphore_signal(barrier, inc=1, device_id={'tp': dev}, device_id_type=MESH)
+    pl.semaphore_wait(barrier, 3)
+
+    my_rows = pl.ds(pl.multiple_of(core * rows, rows), rows)
+    their_rows = pl.ds(pl.multiple_of(other * rows, rows), rows)
+    o_push = remote(o_ref, o_all.at[my_rows, :], pre_send.at[0], pre_recv.at[0], partner)
+    x_push = remote(x_ref.at[:, pl.ds(theirs, half)], x_half.at[my_rows, :], pre_send.at[1], pre_recv.at[1], partner)
+    o_push.start()
+    x_push.start()
+    o_all[my_rows, :] = o_ref[...]
+    x_half[my_rows, :] = x_ref[:, pl.ds(mine, half)]
+    gain = gain_ref[...].astype(f32)
+    gain_top = jnp.maximum(jnp.max(jnp.abs(gain), axis=1, keepdims=True), 1e-30)
+    gain_s[...] = gain / gain_top
+    acc[...] = jnp.zeros_like(acc)
+    ssq[...] = jnp.zeros_like(ssq)
+    remote(o_ref, o_all.at[their_rows, :], pre_send.at[0], pre_recv.at[0], partner).wait_recv()
+    remote(x_ref.at[:, pl.ds(theirs, half)], x_half.at[their_rows, :], pre_send.at[1], pre_recv.at[1], partner).wait_recv()
+
+    def reach(t, d):
+        first = reach_max - lax.rem(t, 2)
+        return first if d == 0 else chips - 1 - first
+
+    def origin(h, d):
+        return lax.rem(chip + chips - h, chips) if d == 0 else lax.rem(chip + h, chips)
+
+    def block(t, src):
+        return x1_all.at[core * tiles + t, pl.ds(pl.multiple_of(src * chip_rows, chip_rows), chip_rows), :]
+
+    def ring_copy(t, src, hop, d):
+        return remote(block(t, src), block(t, src), g_send.at[d, t, hop - 1], g_recv.at[d, t, hop - 1], upper if d == 0 else lower)
+
+    def pair_copy(t, src):
+        return remote(block(t, src), block(t, src), p_send.at[t], p_recv.at[t], partner)
+
+    def produce(t):
+        for q in range(subs):
+            i = t * subs + q
+            slot = lax.rem(i, 2)
+            wo_copy(i).wait()
+            prod = jnp.dot(o_all[...], wo_buf[slot], preferred_element_type=f32)
+            x1 = (x_half[:, pl.ds(pl.multiple_of(i * sub, 128), sub)].astype(f32) + prod).astype(bf16)
+            x1_all[core * tiles + t, pl.ds(pl.multiple_of(chip * chip_rows, chip_rows), chip_rows), pl.ds(q * sub, sub)] = x1
+
+            @pl.when(i + 2 < tiles * subs)
+            def _():
+                wo_copy(i + 2).start()
+        for d in range(2):
+            ring_copy(t, chip, 1, d).start()
+        pair_copy(t, chip).start()
+
+    def forward(t, h):
+        for d in range(2):
+            @pl.when(h <= reach(t, d))
+            def _():
+                src = origin(h, d)
+                ring_copy(t, src, h, d).wait_recv()
+
+                @pl.when(h < reach(t, d))
+                def _():
+                    ring_copy(t, src, h + 1, d).start()
+                pair_copy(t, src).start()
+
+    def consume(t):
+        slot = lax.rem(t, 2)
+        whole = x1_all.at[other * tiles + t]
+        remote(whole, whole, p_send.at[t], p_recv.at[t], partner).wait_recv()
+        for h in range(2):
+            @pl.loop(0, chips)
+            def _(b):
+                rs = pl.ds(pl.multiple_of(b * chip_rows, chip_rows), chip_rows)
+                vals = x1_all[h * tiles + t, rs, :].astype(f32)
+                sq = vals * vals
+                tot = sq[:, 0:128]
+                for k in range(1, tile // 128):
+                    tot += sq[:, k * 128:(k + 1) * 128]
+                ssq[rs, :] += tot
+                xg[rs, h * tile:(h + 1) * tile] = (vals * gain_s[:, pl.ds(pl.multiple_of(h * half + t * tile, 128), tile)]).astype(bf16)
+        for copy in wgu_copies(t):
+            copy.wait()
+
+        @pl.loop(0, 2 * ffn // 256)
+        def _(i):
+            cs = pl.ds(pl.multiple_of(i * 256, 256), 256)
+            acc[:, cs] += jnp.dot(xg[...], wgu_buf[slot, :, cs], preferred_element_type=f32)
+
+    last_hop = GATHER_LAG * reach_max
+
+    def gather_round(j, carry):
+        @pl.when(j < tiles)
+        def _():
+            produce(j)
+        for h in range(1, reach_max + 1):
+            t = j - GATHER_LAG * h
+
+            @pl.when((t >= 0) & (t < tiles))
+            def _():
+                forward(t, h)
+        t_use = j - last_hop - 1
+
+        @pl.when((t_use >= 0) & (t_use < tiles))
+        def _():
+            consume(t_use)
+        t_next = j - last_hop + 1
+
+        @pl.when((t_next >= 0) & (t_next < tiles))
+        def _():
+            for copy in wgu_copies(t_next):
+                copy.start()
+
+        @pl.when((t_next >= 0) & (t_next < tiles))
+        def _():
+            wd_copy(t_next).start()
+            wd_push(t_next).start()
+        return carry
+
+    lax.fori_loop(0, tiles + last_hop + 1, gather_round, 0)
+
+    act_mine = pl.ds(pl.multiple_of(core * ffn, 128), ffn)
+    act_theirs = pl.ds(pl.multiple_of(other * ffn, 128), ffn)
+
+    def act_copy(b):
+        ref = act_all.at[pl.ds(pl.multiple_of(b * chip_rows, chip_rows), chip_rows), act_mine]
+        return remote(ref, ref, a_send.at[b], a_recv.at[b], partner)
+
+    def act_arrival(b):
+        ref = act_all.at[pl.ds(pl.multiple_of(b * chip_rows, chip_rows), chip_rows), act_theirs]
+        return remote(ref, ref, a_send.at[b], a_recv.at[b], partner)
+
+    @pl.loop(0, chips)
+    def _(b):
+        rs = pl.ds(pl.multiple_of(b * chip_rows, chip_rows), chip_rows)
+        inv = lax.rsqrt(jnp.sum(ssq[rs, :], axis=1, keepdims=True) / width + EPS)
+        gate = acc[rs, 0:ffn] * inv * gain_top
+        upv = acc[rs, ffn:2 * ffn] * inv * gain_top
+        act_all[rs, act_mine] = (gate / (1.0 + jnp.exp(-gate)) * upv).astype(bf16)
+        act_copy(b).start()
+
+    @pl.loop(0, chips)
+    def _(b):
+        act_arrival(b).wait_recv()
+
+    ring_bufs = (ring_up, ring_dn)
+    stage_bufs = (stage_up, stage_dn)
+
+    def rows_of(c):
+        return pl.ds(pl.multiple_of(c * chip_rows, chip_rows), chip_rows)
+
+    def sum_copy(t, s, d):
+        src = stage_bufs[d].at[t] if s == 1 else ring_bufs[d].at[t, s - 2]
+        return remote(src, ring_bufs[d].at[t, s - 1], r_send.at[d, t, s - 1], r_recv.at[d, t, s - 1], upper if d == 0 else lower)
+
+    def target(t, s, d):
+        ahead = reach(t, d) - s + 1
+        return lax.rem(chip + ahead, chips) if d == 0 else lax.rem(chip + chips - ahead, chips)
+
+    def out_copy(t):
+        return remote(stage_out.at[t], out_ref.at[:, pl.ds(pl.multiple_of(mine + t * tile, 128), tile)], f_send.at[t], f_recv.at[t], partner)
+
+    def out_arrival(t):
+        return remote(stage_out.at[t], out_ref.at[:, pl.ds(pl.multiple_of(theirs + t * tile, 128), tile)], f_send.at[t], f_recv.at[t], partner)
+
+    def finish(t):
+        slot = lax.rem(t, depth)
+        for d in range(2):
+            for s in range(1, reach_max + 1):
+                @pl.when(s == reach(t, d))
+                def _():
+                    sum_copy(t, s, d).wait_recv()
+
+        def total(c):
+            near = pl.ds(pl.multiple_of(c * rows, rows), rows)
+            far = pl.ds(pl.multiple_of(chip * chip_rows + c * rows, rows), rows)
+            val = part[slot, far, :]
+            for d in range(2):
+                val += ring_bufs[d][t, reach(t, d) - 1, near, :].astype(f32)
+            return (x1_all[core * tiles + t, far, :].astype(f32) + val).astype(bf16)
+
+        stage_out[t] = total(other)
+        out_copy(t).start()
+        out_ref[:, pl.ds(pl.multiple_of(mine + t * tile, 128), tile)] = total(core)
+
+    def scatter_round(j, carry):
+        @pl.when(j < tiles)
+        def _():
+            slot = lax.rem(j, depth)
+            wd_copy(j).wait()
+            wd_arrival(j).wait_recv()
+
+            @pl.loop(0, tile // 256)
+            def _(i):
+                cs = pl.ds(pl.multiple_of(i * 256, 256), 256)
+                part[slot, :, cs] = jnp.dot(act_all[...], wd_all[j, :, cs], preferred_element_type=f32)
+            for d in range(2):
+                stage_bufs[d][j] = part[slot, rows_of(target(j, 1, d)), :].astype(bf16)
+                sum_copy(j, 1, d).start()
+        for s in range(2, reach_max + 1):
+            t = j - SCATTER_LAG * (s - 1)
+
+            @pl.when((t >= 0) & (t < tiles))
+            def _():
+                for d in range(2):
+                    @pl.when(s <= reach(t, d))
+                    def _():
+                        sum_copy(t, s - 1, d).wait_recv()
+                        buf = ring_bufs[d]
+                        own = part[lax.rem(t, depth), rows_of(target(t, s, d)), :]
+                        buf[t, s - 2] = (buf[t, s - 2].astype(f32) + own).astype(bf16)
+                        sum_copy(t, s, d).start()
+        t_end = j - SCATTER_LAG * reach_max
+
+        @pl.when((t_end >= 0) & (t_end < tiles))
+        def _():
+            finish(t_end)
+        return carry
+
+    lax.fori_loop(0, tiles + SCATTER_LAG * reach_max, scatter_round, 0)
+
+    o_push.wait_send()
+    x_push.wait_send()
+
+    @pl.loop(0, chips)
+    def _(b):
+        act_copy(b).wait_send()
+
+    @pl.loop(0, tiles)
+    def _(t):
+        out_arrival(t).wait_recv()
+        out_copy(t).wait_send()
+        wd_push(t).wait_send()
+        whole = x1_all.at[core * tiles + t]
+        remote(whole, whole, p_send.at[t], p_recv.at[t], partner).wait_send()
+        for d in range(2):
+            for h in range(1, reach_max + 1):
+                @pl.when(h <= reach(t, d))
+                def _():
+                    ring_copy(t, chip, h, d).wait_send()
+                    sum_copy(t, h, d).wait_send()
+
+
+def fused_tail(n, head_out, hidden, mlp_norm, w_out, w_gate, w_up, w_down, tile=512, sub=256):
+    bf16, f32 = jnp.bfloat16, jnp.float32
+    rows, width = hidden.shape
+    inner = head_out.shape[1]
+    ffn = w_gate.shape[1]
+    half = width // 2
+    tiles = half // tile
+    chips = n // 2
+    reach = chips // 2
+    group = rows * n
+    depth = min(tiles, SCATTER_LAG * reach + 1)
+    dma = pltpu.SemaphoreType.DMA
+    vmem = pl.BlockSpec(memory_space=pltpu.VMEM)
+    hbm = pl.BlockSpec(memory_space=pl.ANY)
+    scratch = [
+        pltpu.VMEM((2 * rows, inner), bf16),
+        pltpu.VMEM((2 * rows, half), bf16),
+        pltpu.VMEM((1, width), f32),
+        pltpu.VMEM((2, inner, sub), bf16),
+        pltpu.VMEM((2, 2 * tile, 2 * ffn), bf16),
+        pltpu.VMEM((2 * tiles, group, tile), bf16),
+        pltpu.VMEM((group, 2 * tile), bf16),
+        pltpu.VMEM((group, 2 * ffn), f32),
+        pltpu.VMEM((group, 128), f32),
+        pltpu.VMEM((group, 2 * ffn), bf16),
+        pltpu.VMEM((tiles, 2 * ffn, tile), bf16),
+        pltpu.VMEM((depth, group, tile), f32),
+        pltpu.VMEM((tiles, 2 * rows, tile), bf16),
+        pltpu.VMEM((tiles, 2 * rows, tile), bf16),
+        pltpu.VMEM((tiles, reach, 2 * rows, tile), bf16),
+        pltpu.VMEM((tiles, reach, 2 * rows, tile), bf16),
+        pltpu.VMEM((tiles, rows, tile), bf16),
+        dma((2,)), dma((2,)), dma((2,)), dma((2, 4)), dma((tiles,)), dma((tiles,)), dma((tiles,)),
+        dma((2, tiles, reach)), dma((2, tiles, reach)), dma((tiles,)), dma((tiles,)),
+        dma((chips,)), dma((chips,)), dma((2, tiles, reach)), dma((2, tiles, reach)), dma((tiles,)), dma((tiles,)),
+    ]
+    return pl.pallas_call(
+        functools.partial(tail_kernel, n, tile, sub),
+        out_shape=jax.ShapeDtypeStruct((rows, width), bf16),
+        in_specs=[vmem, vmem, vmem, hbm, hbm, hbm, hbm],
+        out_specs=vmem,
+        scratch_shapes=scratch,
+        compiler_params=pltpu.CompilerParams(collective_id=0, has_side_effects=True, vmem_limit_bytes=67_043_328),
+        name='tail',
+    )(head_out, hidden, mlp_norm.reshape(1, width), w_out, w_gate, w_up, w_down)
 
 
 def solution(mesh):
@@ -70,15 +418,8 @@
     out_specs = (rows_spec, rows_spec, rows_spec)
 
     def device_step(hidden, cache_lat, cache_rope, seq_lens, attn_norm, w_query, w_kv_down, kv_norm, w_key_up, w_val_up, w_out, mlp_norm, w_gate, w_up, w_down):
-        resid, lat_new, rope_new = attention_block(hidden, cache_lat, cache_rope, seq_lens, attn_norm, w_query, w_kv_down, kv_norm, w_key_up, w_val_up, w_out)
-        mlp_in = rms_norm(resid, mlp_norm)
-        group_in = lax.all_gather(mlp_in, 'tp', axis=0, tiled=True)
-        gate_proj = jnp.dot(group_in, w_gate, preferred_element_type=jnp.float32)
-        up_proj = jnp.dot(group_in, w_up, preferred_element_type=jnp.float32)
-        act = (jax.nn.silu(gate_proj) * up_proj).astype(jnp.bfloat16)
-        partial_out = jnp.dot(act, w_down, preferred_element_type=jnp.float32).astype(jnp.bfloat16)
-        mlp_out = lax.psum_scatter(partial_out, 'tp', scatter_dimension=0, tiled=True)
-        out_hidden = (resid.astype(jnp.float32) + mlp_out.astype(jnp.float32)).astype(jnp.bfloat16)
+        head_out, lat_new, rope_new = attention_block(hidden, cache_lat, cache_rope, seq_lens, attn_norm, w_query, w_kv_down, kv_norm, w_key_up, w_val_up)
+        out_hidden = fused_tail(mesh.shape['tp'], head_out, hidden, mlp_norm, w_out, w_gate, w_up, w_down)
         return out_hidden, lat_new, rope_new
 
     return jax.shard_map(device_step, mesh=mesh, in_specs=in_specs, out_specs=out_specs, check_vma=False)

time: 307 us -> 221 us (0.72)
  Pallas kernels: 0 us -> 125 us
  waiting for transfers between devices: 113 us -> 0 us
  matrix products: 167 us -> 84.9 us
  between operations: 14.3 us -> 0.85 us
  other arithmetic: 8.74 us -> 5.23 us
  local copies, waits for them, and re-layouts: 1.42 us -> 4.74 us
    pallas_call x0 -> x1, Pallas kernels: none -> 125 us  [fused_tail(): pl.pallas_call(functools.partial(tail_kernel, n, tile, sub), out_shape=ja...]
    dot_general x4 -> x0, matrix products: 83 us -> none  [the longest x1 39.7 us: attention_block(): attn_out = jnp.dot(head_out, w_out, preferred_element_type=jnp.float32)]
    reduce_scatter x1 -> x0, waiting for transfers between devices: 60.3 us -> none  [device_step(): lax.psum_scatter(partial_out, 'tp', scatter_dimension=0, tiled=True)]
    all_gather x1 -> x0, waiting for transfers between devices: 52.7 us -> none  [device_step(): group_in = lax.all_gather(mlp_in, 'tp', axis=0, tiled=True)]
  transfers between devices with their start and end apart: 2 -> 0, of which waited for: 2 -> 0; matrix products, arithmetic and copies ran while one was open for 0% -> 0% of each run, Pallas kernels for 0% -> 0%
where the time goes in v1:
time: 221 us
  Pallas kernels  125 us (57%)
  matrix products  84.9 us (38%)
  other arithmetic  5.23 us (2%)
  local copies, waits for them, and re-layouts  4.74 us (2%)
    pallas_call x1, Pallas kernels, fused_tail(): pl.pallas_call(functools.partial(tail_kernel, n, tile, sub), out_shape=ja...  125 us
    dot_general x1, matrix products, attention_block(): jnp.dot(normed, w_query, preferred_element_type=jnp.float32)  56.7 us
    dot_general x1, matrix products, attention_block(): jnp.einsum('bhk,khv->bhv', lat_out, val_up, preferred_element_type=jnp.fl...  8.34 us
    dot_general x1, matrix products, attention_block(): jnp.einsum('bhn,khn->bhk', query[:, :, :NOPE_DIM], key_up, preferred_elem...  6.53 us
    dot_general x1, matrix products, attention_block(): jnp.dot(normed, w_kv_down, preferred_element_type=jnp.float32)  6.04 us

profile of v1, /device:TPU:21, one launch (start us, length us, event | category | flops | bytes accessed | tf_op | source)
XLA Modules:
  0.0 221.0 jit_solution(13235987258055930373)
XLA Ops:
  0.6 0.7 convert_element_type.63
  1.3 1.2 fusion.36
  2.6 6.0 %convolution_convert_fusion.1 = bf16[32,576]{1,0:T(8,128)(2,1)S(1)} fusion(bf16[7168,576]{0,1:T(8,128)(2,1)} %param.21, bf16[32,7168]{1,0:T(8,128)(2,1)} %x_ref.1, f32[7168]{0:T(1024)S(1)} %convert_element_type.63, f32[32]{0:T(128)S(1)} %add_rsqrt_fusion.1), kind=kOutput, calls=%fused_computation.23 | convolution fusion | flops 265177088 | bytes 8781952 | tf_op jit(solution)/shard_map/dot_general | solution.py:42
  8.7 0.1 subtract_convert_fusion.1
  8.9 56.7 %convolution_convert_fusion = bf16[32,12288]{1,0:T(8,128)(2,1)S(1)} fusion(bf16[7168,12288]{1,0:T(8,128)(2,1)} %param.20, bf16[32,7168]{1,0:T(8,128)(2,1)S(1)} %copy-done.1, f32[7168]{0:T(1024)S(1)} %convert_element_type.63, f32[32]{0:T(128)S(1)} %add_rsqrt_fusion.1), kind=kOutput, calls=%fused_computation | convolution fusion | flops 5638455296 | bytes 177434752 | tf_op jit(solution)/shard_map/dot_general | solution.py:41
  65.5 1.2 reshape.116
  66.7 0.1 slice_convert_fusion
  66.8 0.6 subtract_convert_fusion
  67.5 0.4 fusion.45
  68.0 0.4 fusion.46
  68.4 0.1 slice.32
  68.5 6.5 %convert_bitcast_fusion = bf16[32,64,512]{2,0,1:T(8,128)(2,1)S(1)} fusion(bf16[32,64,128]{2,1,0:T(8,128)(2,1)S(1)} %slice.32, bf16[512,8192]{1,0:T(8,128)(2,1)} %param.23), kind=kOutput, calls=%fused_computation.11 | convolution fusion | flops 269484032 | bytes 11010048 | tf_op jit(solution)/shard_map/bhn,khn->bhk/dot_general | solution.py:48
  75.0 0.1 iota_compare_fusion
  75.1 2.7 %fusion.59 = (f32[32,64]{1,0:T(8,128)S(1)}, f32[32,64,128]{2,1,0:T(8,128)S(1)}) fusion(f32[32,64,128]{2,1,0:T(8,128)S(1)} %fusion.46, bf16[32,128,512]{2,1,0:T(8,128)(2,1)S(1)} %copy-done, bf16[32,64,512]{2,0,1:T(8,128)(2,1)S(1)} %convert_bitcast_fusion, pred[32,128]{1,0:T(8,128)(4,1)S(1)} %iota_compare_fusion), kind=kOutput, calls=%fused_computation.67 | convolution fusion | flops 269481984 | bytes 8400896 | tf_op jit(solution)/shard_map/bhk,bsk->bhs/dot_general | solution.py:49
  77.9 0.1 fusion.47
  78.1 1.2 fusion.12
  79.4 0.7 fusion.35
  80.1 2.5 %fusion.39 = f32[32,64,512]{2,1,0:T(8,128)} fusion(bf16[32,128,512]{2,1,0:T(8,128)(2,1)S(1)} %copy-done, f32[32,64,128]{2,1,0:T(8,128)S(1)} %get-tuple-element.14, f32[32,64]{1,0:T(8,128)S(1)} %get-tuple-element.8, f32[32,64]{1,0:T(8,128)S(1)} %fusion.53), kind=kOutput, calls=%fused_computation.32 | convolution fusion | flops 269221888 | bytes 9453568 | tf_op jit(solution)/shard_map/bhs,bsk->bhk/dot_general | solution.py:60
  82.6 8.3 %fusion.30 = bf16[64,4,8,128]{3,2,1,0:T(8,128)(2,1)S(1)} fusion(f32[32,64,512]{2,1,0:T(8,128)} %fusion.39, f32[32,512]{1,0:T(8,128)S(1)} %get-tuple-element.3, f32[32,64]{0,1:T(8,128)S(1)} %copy.21, bf16[512,8192]{1,0:T(8,128)(2,1)} %param.24), kind=kOutput, calls=%fused_computation.20 | convolution fusion | flops 271843328 | bytes 13180928 | tf_op jit(solution)/shard_map/bhk,khv->bhv/dot_general | solution.py:63
  91.0 0.9 copy.74
  91.9 0.6 reshape.120.gain_ref
  92.5 125.3 %tail.1 = bf16[32,7168]{1,0:T(8,128)(2,1)} custom-call(bf16[32,8192]{1,0:T(8,128)(2,1)} %bitcast.41, bf16[32,7168]{1,0:T(8,128)(2,1)} %x_ref.1, bf16[1,7168]{1,0:T(2,128)(2,1)} %reshape.120.gain_ref, bf16[8192,7168]{1,0:T(8,128)(2,1)} %wo_hbm.1, bf16[7168,1152]{1,0:T(8,128)(2,1)} %wg_hbm.1, bf16[7168,1152]{1,0:T(8,128)(2,1)} %wu_hbm.1, bf16[1152,7168]{1,0:T(8,128)(2,1)} %wd_hbm.1), custom_call_target="tpu_custom_call" | custom-call | tf_op jit(solution)/shard_map/tail/pallas_call | solution.py:402
  217.8 1.4 pad_maximum_fusion.3
  219.2 1.8 copy.76
  (29 shorter events, 0.4 us)
Async XLA Ops:
  2.6 6.1 %copy-start.8 = (s32[32]{0:T(128)S(1)}, s32[32]{0:T(128)}, u32[]{:S(2)}) copy-start(s32[32]{0:T(128)} %param.18) | copy-start | bytes 388
  2.6 6.3 %copy-start.1 = (bf16[32,7168]{1,0:T(8,128)(2,1)S(1)}, bf16[32,7168]{1,0:T(8,128)(2,1)}, u32[]{:S(2)}) copy-start(bf16[32,7168]{1,0:T(8,128)(2,1)} %x_ref.1) | copy-start | bytes 1376260
  8.8 58.6 %copy-start.3 = (bf16[32,32]{1,0:T(8,128)(2,1)}, bf16[32,32]{1,0:T(8,128)(2,1)S(1)}, u32[]{:S(2)}) copy-start(bf16[32,32]{1,0:T(8,128)(2,1)S(1)} %get-tuple-element.9) | copy-start | bytes 6148
  8.8 58.6 %copy-start.4 = (bf16[32,32]{1,0:T(8,128)(2,1)}, bf16[32,32]{1,0:T(8,128)(2,1)S(1)}, u32[]{:S(2)}) copy-start(bf16[32,32]{1,0:T(8,128)(2,1)S(1)} %get-tuple-element.10) | copy-start | bytes 6148
  65.5 2.4 %copy-start.2 = (bf16[32,128,64]{1,2,0:T(8,128)(2,1)S(1)}, bf16[32,128,64]{1,2,0:T(8,128)(2,1)}, u32[]{:S(2)}) copy-start(bf16[32,128,64]{1,2,0:T(8,128)(2,1)} %param.17) | copy-start | bytes 1572868
  68.5 6.6 %copy-start = (bf16[32,128,512]{2,1,0:T(8,128)(2,1)S(1)}, bf16[32,128,512]{2,1,0:T(8,128)(2,1)}, u32[]{:S(2)}) copy-start(bf16[32,128,512]{2,1,0:T(8,128)(2,1)} %param.16) | copy-start | bytes 12582916
  75.1 2.9 %copy-start.7 = (bf16[512]{0:T(512)(128)(2,1)S(1)}, bf16[512]{0:T(512)(128)(2,1)}, u32[]{:S(2)}) copy-start(bf16[512]{0:T(512)(128)(2,1)} %param.22) | copy-start | bytes 3076
  78.1 4.4 %copy-start.5 = (bf16[32,512]{1,0:T(8,128)(2,1)}, bf16[32,512]{1,0:T(8,128)(2,1)S(1)}, u32[]{:S(2)}) copy-start(bf16[32,512]{1,0:T(8,128)(2,1)S(1)} %get-tuple-element.19) | copy-start | bytes 98308
  82.6 9.2 %copy-start.6 = (bf16[7168]{0:T(1024)(128)(2,1)S(1)}, bf16[7168]{0:T(1024)(128)(2,1)}, u32[]{:S(2)}) copy-start(bf16[7168]{0:T(1024)(128)(2,1)} %param.26) | copy-start | bytes 43012

commit v2 on v1

--- a/solution.py
+++ b/solution.py
@@ -37,9 +37,8 @@
 def attention_block(hidden, cache_lat, cache_rope, seq_lens, attn_norm, w_query, w_kv_down, kv_norm, w_key_up, w_val_up):
     rows = hidden.shape[0]
     heads = w_key_up.shape[1] // NOPE_DIM
-    normed = rms_norm(hidden, attn_norm)
-    query = jnp.dot(normed, w_query, preferred_element_type=jnp.float32).astype(jnp.bfloat16).reshape(rows, heads, NOPE_DIM + ROPE_DIM)
-    kv_proj = jnp.dot(normed, w_kv_down, preferred_element_type=jnp.float32).astype(jnp.bfloat16)
+    query, kv_proj = paired_query(hidden, attn_norm, w_query, w_kv_down)
+    query = query.reshape(rows, heads, NOPE_DIM + ROPE_DIM)
     lat_new = rms_norm(kv_proj[:, :value_a7], kv_norm)
     cos_tab, sin_tab = rope_tables(seq_lens)
     rope_new = rotate(kv_proj[:, value_a7:].astype(jnp.float32), cos_tab, sin_tab).astype(jnp.bfloat16)
@@ -64,8 +63,125 @@
     return head_out, lat_new, rope_new
 
 MESH = pl.DeviceIdType.MESH
-GATHER_LAG = 1
-SCATTER_LAG = 1
+GATHER_LAG = 2
+SCATTER_LAG = 2
+
+def query_kernel(sub, x_ref, gain_ref, wq_hbm, wkv_hbm, q_ref, kv_ref,
+                 h_all, w_buf, wkv_buf, stage, kv_part, kv_stage, kv_in,
+                 w_sem, wkv_sem, h_send, h_recv, k_send, k_recv, q_send, q_recv):
+    f32, bf16 = jnp.float32, jnp.bfloat16
+    rows, width = x_ref.shape
+    half = width // 2
+    q_half = wq_hbm.shape[1] // 2
+    tiles = q_half // sub
+    slots = w_buf.shape[0]
+    me = lax.axis_index('tp')
+    core = lax.rem(me, 2)
+    other = 1 - core
+    partner = me + 1 - 2 * core
+    my_rows = pl.ds(pl.multiple_of(core * rows, rows), rows)
+    their_rows = pl.ds(pl.multiple_of(other * rows, rows), rows)
+    my_depth = pl.ds(pl.multiple_of(core * half, 128), half)
+
+    def remote(src, dst, send_sem, recv_sem):
+        return pltpu.make_async_remote_copy(src_ref=src, dst_ref=dst, send_sem=send_sem, recv_sem=recv_sem, device_id={'tp': partner}, device_id_type=MESH)
+
+    def w_copy(i):
+        slot = lax.rem(i, slots)
+        return pltpu.make_async_copy(wq_hbm.at[:, pl.ds(pl.multiple_of(core * q_half + i * sub, 128), sub)], w_buf.at[slot], w_sem.at[slot])
+
+    wkv_copy = pltpu.make_async_copy(wkv_hbm.at[my_depth, :], wkv_buf, wkv_sem.at[0])
+    wkv_copy.start()
+    for i in range(slots):
+        w_copy(i).start()
+
+    barrier = pltpu.get_barrier_semaphore()
+    pl.semaphore_signal(barrier, inc=1, device_id={'tp': partner}, device_id_type=MESH)
+
+    step = min(1024, width)
+    tot = jnp.zeros((rows, 128), f32)
+    for c in range(0, width, step):
+        vals = x_ref[:, c:c + step].astype(f32)
+        sq = vals * vals
+        for k in range(0, step, 128):
+            tot += sq[:, k:k + 128]
+    inv = lax.rsqrt(jnp.sum(tot, axis=1, keepdims=True) / width + EPS)
+    for c in range(0, width, step):
+        vals = x_ref[:, c:c + step].astype(f32)
+        h_all[my_rows, c:c + step] = (vals * inv * gain_ref[:, c:c + step].astype(f32)).astype(bf16)
+
+    pl.semaphore_wait(barrier, 1)
+    h_push = remote(h_all.at[my_rows, :], h_all.at[my_rows, :], h_send.at[0], h_recv.at[0])
+    h_push.start()
+    remote(h_all.at[their_rows, :], h_all.at[their_rows, :], h_send.at[0], h_recv.at[0]).wait_recv()
+
+    wkv_copy.wait()
+    kv_part[...] = jnp.dot(h_all[:, my_depth], wkv_buf[...], preferred_element_type=f32)
+    kv_stage[...] = kv_part[their_rows, :]
+    kv_push = remote(kv_stage, kv_in, k_send.at[0], k_recv.at[0])
+    kv_push.start()
+
+    def cols_of(c, i):
+        return pl.ds(pl.multiple_of(c * q_half + i * sub, 128), sub)
+
+    def q_copy(i):
+        return remote(stage.at[i], q_ref.at[:, cols_of(core, i)], q_send.at[i], q_recv.at[i])
+
+    @pl.loop(0, tiles)
+    def _(i):
+        slot = lax.rem(i, slots)
+        w_copy(i).wait()
+        prod = jnp.dot(h_all[...], w_buf[slot], preferred_element_type=f32).astype(bf16)
+
+        @pl.when(i + slots < tiles)
+        def _():
+            w_copy(i + slots).start()
+        low, high = prod[0:rows], prod[rows:2 * rows]
+        first = core == 0
+        q_ref[:, cols_of(core, i)] = jnp.where(first, low, high)
+        stage[i] = jnp.where(first, high, low)
+        q_copy(i).start()
+
+    kv_push.wait_recv()
+    kv_ref[...] = (kv_part[my_rows, :] + kv_in[...]).astype(bf16)
+    h_push.wait_send()
+    kv_push.wait_send()
+
+    @pl.loop(0, tiles)
+    def _(i):
+        q_copy(i).wait_send()
+        remote(stage.at[i], q_ref.at[:, cols_of(other, i)], q_send.at[i], q_recv.at[i]).wait_recv()
+
+
+def paired_query(hidden, attn_norm, w_query, w_kv_down, sub=256):
+    bf16, f32 = jnp.bfloat16, jnp.float32
+    rows, width = hidden.shape
+    q_cols = w_query.shape[1]
+    kv_cols = w_kv_down.shape[1]
+    tiles = q_cols // 2 // sub
+    slots = min(8, tiles)
+    dma = pltpu.SemaphoreType.DMA
+    vmem = pl.BlockSpec(memory_space=pltpu.VMEM)
+    hbm = pl.BlockSpec(memory_space=pl.ANY)
+    scratch = [
+        pltpu.VMEM((2 * rows, width), bf16),
+        pltpu.VMEM((slots, width, sub), bf16),
+        pltpu.VMEM((width // 2, kv_cols), bf16),
+        pltpu.VMEM((tiles, rows, sub), bf16),
+        pltpu.VMEM((2 * rows, kv_cols), f32),
+        pltpu.VMEM((rows, kv_cols), f32),
+        pltpu.VMEM((rows, kv_cols), f32),
+        dma((slots,)), dma((1,)), dma((1,)), dma((1,)), dma((1,)), dma((1,)), dma((tiles,)), dma((tiles,)),
+    ]
+    return pl.pallas_call(
+        functools.partial(query_kernel, sub),
+        out_shape=(jax.ShapeDtypeStruct((rows, q_cols), bf16), jax.ShapeDtypeStruct((rows, kv_cols), bf16)),
+        in_specs=[vmem, vmem, hbm, hbm],
+        out_specs=(vmem, vmem),
+        scratch_shapes=scratch,
+        compiler_params=pltpu.CompilerParams(collective_id=1, has_side_effects=True, vmem_limit_bytes=60_000_000),
+        name='query',
+    )(hidden, attn_norm.reshape(1, width), w_query, w_kv_down)
 
 
 def tail_kernel(n, tile, sub, o_ref, x_ref, gain_ref, wo_hbm, wg_hbm, wu_hbm, wd_hbm, out_ref,
@@ -363,7 +479,7 @@
                     sum_copy(t, h, d).wait_send()
 
 
-def fused_tail(n, head_out, hidden, mlp_norm, w_out, w_gate, w_up, w_down, tile=512, sub=256):
+def fused_tail(n, head_out, hidden, mlp_norm, w_out, w_gate, w_up, w_down, tile=256, sub=256):
     bf16, f32 = jnp.bfloat16, jnp.float32
     rows, width = hidden.shape
     inner = head_out.shape[1]

time: 221 us -> 208 us (0.941)
  matrix products: 84.9 us -> 18.7 us
  Pallas kernels: 125 us -> 164 us
  local copies, waits for them, and re-layouts: 4.74 us -> 20.5 us
    dot_general x2 -> x0, matrix products: 62.7 us -> none  [the longest x1 56.7 us: attention_block(): jnp.dot(normed, w_query, preferred_element_type=jnp.float32)]
    pallas_call x0 -> x1, Pallas kernels: none -> 38.1 us  [paired_query(): pl.pallas_call(functools.partial(query_kernel, sub), out_shape=(jax.Shape...]
    unnamed x19 -> x24, local copies, waits for them, and re-layouts: 1.86 us -> 15.9 us
    dot_general x1, matrix products: 6.53 us -> 2.96 us  [attention_block(): jnp.einsum('bhn,khn->bhk', query[:, :, :NOPE_DIM], key_up, preferred_elem...]
where the time goes in v2:
time: 208 us
  Pallas kernels  164 us (79%)
  local copies, waits for them, and re-layouts  20.5 us (10%)
  matrix products  18.7 us (9%)
  other arithmetic  4.03 us (2%)
    pallas_call x1, Pallas kernels, fused_tail(): pl.pallas_call(functools.partial(tail_kernel, n, tile, sub), out_shape=ja...  126 us
    pallas_call x1, Pallas kernels, paired_query(): pl.pallas_call(functools.partial(query_kernel, sub), out_shape=(jax.Shape...  38.1 us
    unnamed x24, local copies, waits for them, and re-layouts  15.9 us
    dot_general x1, matrix products, attention_block(): jnp.einsum('bhk,khv->bhv', lat_out, val_up, preferred_element_type=jnp.fl...  8.21 us

profile of v2, /device:TPU:21, one launch (start us, length us, event | category | flops | bytes accessed | tf_op | source)
XLA Modules:
  0.0 207.7 jit_solution(11262580656711074184)
XLA Ops:
  0.6 12.4 %copy.18.wkv_hbm = bf16[7168,576]{1,0:T(8,128)(2,1)} copy(bf16[7168,576]{0,1:T(8,128)(2,1)} %param.21) | data formatting | bytes 16515072 | tf_op args[6]
  13.1 0.6 reshape.110.gain_ref
  13.7 38.1 %query.1 = (bf16[32,12288]{1,0:T(8,128)(2,1)}, bf16[32,576]{1,0:T(8,128)(2,1)}) custom-call(bf16[32,7168]{1,0:T(8,128)(2,1)} %x_ref.3, bf16[1,7168]{1,0:T(2,128)(2,1)} %reshape.110.gain_ref, bf16[7168,12288]{1,0:T(8,128)(2,1)} %wq_hbm.1, bf16[7168,576]{1,0:T(8,128)(2,1)} %copy.18.wkv_hbm), custom_call_target="tpu_custom_call" | custom-call | tf_op jit(solution)/shard_map/query/pallas_call | solution.py:176
  51.8 0.8 slice_convert_fusion.1
  52.6 0.1 subtract_convert_fusion.1
  52.8 2.3 %reshape.111 = bf16[32,64,192]{2,1,0:T(8,128)(2,1)S(1)} reshape(bf16[32,12288]{1,0:T(8,128)(2,1)} %get-tuple-element.5) | data formatting | bytes 1572864 | tf_op jit(solution)/shard_map/reshape | solution.py:41
  55.1 0.1 slice_convert_fusion
  55.2 0.6 subtract_convert_fusion
  55.8 0.4 fusion.40
  56.3 0.4 fusion.41
  56.7 0.1 slice.32
  56.8 1.6 copy-done.1
  58.4 3.0 %convert_bitcast_fusion = bf16[32,64,512]{2,0,1:T(8,128)(2,1)S(1)} fusion(bf16[32,64,128]{2,1,0:T(8,128)(2,1)S(1)} %slice.32, bf16[512,8192]{1,0:T(8,128)(2,1)S(1)} %copy-done.1), kind=kOutput, calls=%fused_computation.10 | convolution fusion | flops 269484032 | bytes 11010048 | tf_op jit(solution)/shard_map/bhn,khn->bhk/dot_general | solution.py:47
  61.5 2.7 %fusion.54 = (f32[32,64]{1,0:T(8,128)S(1)}, f32[32,64,128]{2,1,0:T(8,128)S(1)}) fusion(f32[32,64,128]{2,1,0:T(8,128)S(1)} %fusion.41, bf16[32,128,512]{2,1,0:T(8,128)(2,1)S(1)} %copy-done, bf16[32,64,512]{2,0,1:T(8,128)(2,1)S(1)} %convert_bitcast_fusion, pred[32,128]{1,0:T(8,128)(4,1)S(1)} %iota_compare_fusion), kind=kOutput, calls=%fused_computation.59 | convolution fusion | flops 269481984 | bytes 8400896 | tf_op jit(solution)/shard_map/bhk,bsk->bhs/dot_general | solution.py:48
  64.3 0.1 fusion.42
  64.5 1.2 fusion.12
  65.7 0.7 fusion.35
  66.4 2.7 %fusion.36 = f32[32,64,512]{2,1,0:T(8,128)} fusion(bf16[32,128,512]{2,1,0:T(8,128)(2,1)S(1)} %copy-done, f32[32,64,128]{2,1,0:T(8,128)S(1)} %get-tuple-element.18, f32[32,64]{1,0:T(8,128)S(1)} %get-tuple-element.12, f32[32,64]{1,0:T(8,128)S(1)} %fusion.48), kind=kOutput, calls=%fused_computation.25 | convolution fusion | flops 269221888 | bytes 9453568 | tf_op jit(solution)/shard_map/bhs,bsk->bhk/dot_general | solution.py:59
  69.2 8.2 %fusion.30 = bf16[64,4,8,128]{3,2,1,0:T(8,128)(2,1)S(1)} fusion(f32[32,64,512]{2,1,0:T(8,128)} %fusion.36, f32[32,512]{1,0:T(8,128)S(1)} %get-tuple-element.7, f32[32,64]{0,1:T(8,128)S(1)} %copy.22, bf16[512,8192]{1,0:T(8,128)(2,1)} %param.24), kind=kOutput, calls=%fused_computation.19 | convolution fusion | flops 271843328 | bytes 13180928 | tf_op jit(solution)/shard_map/bhk,khv->bhv/dot_general | solution.py:62
  77.4 0.9 copy.75
  78.3 0.6 reshape.115.gain_ref
  78.9 125.6 %tail.1 = bf16[32,7168]{1,0:T(8,128)(2,1)} custom-call(bf16[32,8192]{1,0:T(8,128)(2,1)} %bitcast.38, bf16[32,7168]{1,0:T(8,128)(2,1)} %x_ref.3, bf16[1,7168]{1,0:T(2,128)(2,1)} %reshape.115.gain_ref, bf16[8192,7168]{1,0:T(8,128)(2,1)} %wo_hbm.1, bf16[7168,1152]{1,0:T(8,128)(2,1)} %wg_hbm.1, bf16[7168,1152]{1,0:T(8,128)(2,1)} %wu_hbm.1, bf16[1152,7168]{1,0:T(8,128)(2,1)} %wd_hbm.1), custom_call_target="tpu_custom_call" | custom-call | tf_op jit(solution)/shard_map/tail/pallas_call | solution.py:518
  204.5 1.4 pad_maximum_fusion.3
  205.9 1.8 copy.77
  (31 shorter events, 0.4 us)
Async XLA Ops:
  0.6 12.4 %copy-start.7 = (bf16[7168]{0:T(1024)(128)(2,1)S(1)}, bf16[7168]{0:T(1024)(128)(2,1)}, u32[]{:S(2)}) copy-start(bf16[7168]{0:T(1024)(128)(2,1)} %param.19) | copy-start | bytes 43012
  13.7 38.9 %copy-start.10 = (s32[32]{0:T(128)S(1)}, s32[32]{0:T(128)}, u32[]{:S(2)}) copy-start(s32[32]{0:T(128)} %param.18) | copy-start | bytes 388
  51.8 4.5 %copy-start.2 = (bf16[32,128,64]{1,2,0:T(8,128)(2,1)S(1)}, bf16[32,128,64]{1,2,0:T(8,128)(2,1)}, u32[]{:S(2)}) copy-start(bf16[32,128,64]{1,2,0:T(8,128)(2,1)} %param.17) | copy-start | bytes 1572868
  52.7 4.0 %copy-start.4 = (bf16[32,32]{1,0:T(8,128)(2,1)}, bf16[32,32]{1,0:T(8,128)(2,1)S(1)}, u32[]{:S(2)}) copy-start(bf16[32,32]{1,0:T(8,128)(2,1)S(1)} %get-tuple-element.13) | copy-start | bytes 6148
  52.8 4.0 %copy-start.5 = (bf16[32,32]{1,0:T(8,128)(2,1)}, bf16[32,32]{1,0:T(8,128)(2,1)S(1)}, u32[]{:S(2)}) copy-start(bf16[32,32]{1,0:T(8,128)(2,1)S(1)} %get-tuple-element.14) | copy-start | bytes 6148
  55.1 3.4 %copy-start.1 = (bf16[512,8192]{1,0:T(8,128)(2,1)S(1)}, bf16[512,8192]{1,0:T(8,128)(2,1)}, u32[]{:S(2)}) copy-start(bf16[512,8192]{1,0:T(8,128)(2,1)} %param.23) | copy-start | bytes 25165828
  58.4 3.0 %copy-start = (bf16[32,128,512]{2,1,0:T(8,128)(2,1)S(1)}, bf16[32,128,512]{2,1,0:T(8,128)(2,1)}, u32[]{:S(2)}) copy-start(bf16[32,128,512]{2,1,0:T(8,128)(2,1)} %param.16) | copy-start | bytes 12582916
  61.5 2.8 %copy-start.3 = (bf16[32,576]{1,0:T(8,128)(2,1)S(1)}, bf16[32,576]{1,0:T(8,128)(2,1)}, u32[]{:S(2)}) copy-start(bf16[32,576]{1,0:T(8,128)(2,1)} %get-tuple-element.6) | copy-start | bytes 110596
  61.5 2.9 %copy-start.9 = (bf16[512]{0:T(512)(128)(2,1)S(1)}, bf16[512]{0:T(512)(128)(2,1)}, u32[]{:S(2)}) copy-start(bf16[512]{0:T(512)(128)(2,1)} %param.22) | copy-start | bytes 3076
  64.5 4.6 %copy-start.6 = (bf16[32,512]{1,0:T(8,128)(2,1)}, bf16[32,512]{1,0:T(8,128)(2,1)S(1)}, u32[]{:S(2)}) copy-start(bf16[32,512]{1,0:T(8,128)(2,1)S(1)} %get-tuple-element.23) | copy-start | bytes 98308
  69.2 9.1 %copy-start.8 = (bf16[7168]{0:T(1024)(128)(2,1)S(1)}, bf16[7168]{0:T(1024)(128)(2,1)}, u32[]{:S(2)}) copy-start(bf16[7168]{0:T(1024)(128)(2,1)} %param.26) | copy-start | bytes 43012

commit v3 on v2

--- a/solution.py
+++ b/solution.py
@@ -58,13 +58,34 @@
     prob_new = (expo_new / denom).astype(jnp.bfloat16)
     lat_sum = jnp.einsum('bhs,bsk->bhk', probs, cache_lat, preferred_element_type=jnp.float32) + prob_new.astype(jnp.float32)[..., None] * lat_new.astype(jnp.float32)[:, None, :]
     lat_out = lat_sum.astype(jnp.bfloat16)
-    val_up = w_val_up.reshape(value_a7, heads, -1)
-    head_out = jnp.einsum('bhk,khv->bhv', lat_out, val_up, preferred_element_type=jnp.float32).astype(jnp.bfloat16).reshape(rows, -1)
+    head_out = head_values(jnp.swapaxes(lat_out, 0, 1), w_val_up)
     return head_out, lat_new, rope_new
 
 MESH = pl.DeviceIdType.MESH
-GATHER_LAG = 2
+GATHER_LAG = 1
 SCATTER_LAG = 2
+
+def head_kernel(lat_ref, val_ref, out_ref):
+    heads = lat_ref.shape[0]
+    dim = val_ref.shape[1] // heads
+    for h in range(heads):
+        cols = slice(h * dim, (h + 1) * dim)
+        out_ref[:, cols] = jnp.dot(lat_ref[h], val_ref[:, cols], preferred_element_type=jnp.float32).astype(jnp.bfloat16)
+
+
+def head_values(lat_out, w_val_up, step=8):
+    heads, rows, depth = lat_out.shape
+    cols = w_val_up.shape[1] // heads * step
+    return pl.pallas_call(
+        head_kernel,
+        out_shape=jax.ShapeDtypeStruct((rows, w_val_up.shape[1]), jnp.bfloat16),
+        grid=(heads // step,),
+        in_specs=[pl.BlockSpec((step, rows, depth), lambda i: (i, 0, 0)), pl.BlockSpec((depth, cols), lambda i: (0, i))],
+        out_specs=pl.BlockSpec((rows, cols), lambda i: (0, i)),
+        cost_estimate=pl.CostEstimate(flops=2 * rows * depth * w_val_up.shape[1], bytes_accessed=2 * depth * w_val_up.shape[1], transcendentals=0),
+        name='head_values',
+    )(lat_out, w_val_up)
+
 
 def query_kernel(sub, x_ref, gain_ref, wq_hbm, wkv_hbm, q_ref, kv_ref,
                  h_all, w_buf, wkv_buf, stage, kv_part, kv_stage, kv_in,
@@ -90,7 +111,7 @@
         slot = lax.rem(i, slots)
         return pltpu.make_async_copy(wq_hbm.at[:, pl.ds(pl.multiple_of(core * q_half + i * sub, 128), sub)], w_buf.at[slot], w_sem.at[slot])
 
-    wkv_copy = pltpu.make_async_copy(wkv_hbm.at[my_depth, :], wkv_buf, wkv_sem.at[0])
+    wkv_copy = pltpu.make_async_copy(wkv_hbm.at[:, my_depth], wkv_buf, wkv_sem.at[0])
     wkv_copy.start()
     for i in range(slots):
         w_copy(i).start()
@@ -116,7 +137,7 @@
     remote(h_all.at[their_rows, :], h_all.at[their_rows, :], h_send.at[0], h_recv.at[0]).wait_recv()
 
     wkv_copy.wait()
-    kv_part[...] = jnp.dot(h_all[:, my_depth], wkv_buf[...], preferred_element_type=f32)
+    kv_part[...] = lax.dot_general(h_all[:, my_depth], wkv_buf[...], (((1,), (1,)), ((), ())), preferred_element_type=f32)
     kv_stage[...] = kv_part[their_rows, :]
     kv_push = remote(kv_stage, kv_in, k_send.at[0], k_recv.at[0])
     kv_push.start()
@@ -166,7 +187,7 @@
     scratch = [
         pltpu.VMEM((2 * rows, width), bf16),
         pltpu.VMEM((slots, width, sub), bf16),
-        pltpu.VMEM((width // 2, kv_cols), bf16),
+        pltpu.VMEM((kv_cols, width // 2), bf16),
         pltpu.VMEM((tiles, rows, sub), bf16),
         pltpu.VMEM((2 * rows, kv_cols), f32),
         pltpu.VMEM((rows, kv_cols), f32),
@@ -181,7 +202,7 @@
         scratch_shapes=scratch,
         compiler_params=pltpu.CompilerParams(collective_id=1, has_side_effects=True, vmem_limit_bytes=60_000_000),
         name='query',
-    )(hidden, attn_norm.reshape(1, width), w_query, w_kv_down)
+    )(hidden, attn_norm.reshape(1, width), w_query, w_kv_down.T)
 
 
 def tail_kernel(n, tile, sub, o_ref, x_ref, gain_ref, wo_hbm, wg_hbm, wu_hbm, wd_hbm, out_ref,
@@ -479,7 +500,7 @@
                     sum_copy(t, h, d).wait_send()
 
 
-def fused_tail(n, head_out, hidden, mlp_norm, w_out, w_gate, w_up, w_down, tile=256, sub=256):
+def fused_tail(n, head_out, hidden, mlp_norm, w_out, w_gate, w_up, w_down, tile=512, sub=256):
     bf16, f32 = jnp.bfloat16, jnp.float32
     rows, width = hidden.shape
     inner = head_out.shape[1]

time: 208 us -> 193 us (0.928)
  local copies, waits for them, and re-layouts: 20.5 us -> 7.89 us
  matrix products: 18.7 us -> 10.8 us
  other arithmetic: 4.03 us -> 7.77 us
    unnamed x24 -> x21, local copies, waits for them, and re-layouts: 15.9 us -> 3.47 us
    dot_general x1 -> x0, matrix products: 8.21 us -> none  [attention_block(): jnp.einsum('bhk,khv->bhv', lat_out, val_up, preferred_element_type=jnp.fl...]
    pallas_call x0 -> x1, Pallas kernels: none -> 8.04 us  [head_values(): pl.pallas_call(head_kernel, out_shape=jax.ShapeDtypeStruct((rows, w_val_u...]
    pallas_call x1, Pallas kernels: 126 us -> 119 us  [fused_tail(): pl.pallas_call(functools.partial(tail_kernel, n, tile, sub), out_shape=ja...]
    convert_element_type x0 -> x1, other arithmetic: none -> 3.74 us  [attention_block(): lat_out = lat_sum.astype(jnp.bfloat16)]
where the time goes in v3:
time: 193 us; the launch traced here: 192 us
  Pallas kernels  165 us (85%)
  matrix products  10.8 us (6%)
  local copies, waits for them, and re-layouts  7.89 us (4%)
  other arithmetic  7.77 us (4%)
    pallas_call x1, Pallas kernels, fused_tail(): pl.pallas_call(functools.partial(tail_kernel, n, tile, sub), out_shape=ja...  119 us
    pallas_call x1, Pallas kernels, paired_query(): pl.pallas_call(functools.partial(query_kernel, sub), out_shape=(jax.Shape...  38.4 us
    pallas_call x1, Pallas kernels, head_values(): pl.pallas_call(head_kernel, out_shape=jax.ShapeDtypeStruct((rows, w_val_u...  8.04 us

profile of v3, /device:TPU:21, one launch (start us, length us, event | category | flops | bytes accessed | tf_op | source)
XLA Modules:
  0.0 192.4 jit_solution(13904214721008725527)
XLA Ops:
  0.6 1.3 reshape.104.gain_ref
  2.0 38.4 %query.1 = (bf16[32,12288]{1,0:T(8,128)(2,1)}, bf16[32,576]{1,0:T(8,128)(2,1)}) custom-call(bf16[32,7168]{1,0:T(8,128)(2,1)} %x_ref.3, bf16[1,7168]{1,0:T(2,128)(2,1)} %reshape.104.gain_ref, bf16[7168,12288]{1,0:T(8,128)(2,1)} %wq_hbm.1, bf16[576,7168]{1,0:T(8,128)(2,1)} %bitcast.44), custom_call_target="tpu_custom_call" | custom-call | tf_op jit(solution)/shard_map/query/pallas_call | solution.py:197
  40.4 0.8 slice_convert_fusion.1
  41.2 0.1 subtract_convert_fusion.1
  41.4 2.3 %reshape.105 = bf16[32,64,192]{2,1,0:T(8,128)(2,1)S(1)} reshape(bf16[32,12288]{1,0:T(8,128)(2,1)} %get-tuple-element.5) | data formatting | bytes 1572864 | tf_op jit(solution)/shard_map/reshape | solution.py:41
  43.7 0.1 slice_convert_fusion
  43.8 0.6 subtract_convert_fusion
  44.4 0.4 fusion.24
  44.9 0.4 fusion.25
  45.3 0.1 slice.32
  45.4 1.6 copy-done.1
  47.0 3.0 %convert_bitcast_fusion = bf16[32,64,512]{2,0,1:T(8,128)(2,1)S(1)} fusion(bf16[32,64,128]{2,1,0:T(8,128)(2,1)S(1)} %slice.32, bf16[512,8192]{1,0:T(8,128)(2,1)S(1)} %copy-done.1), kind=kOutput, calls=%fused_computation.5 | convolution fusion | flops 269484032 | bytes 11010048 | tf_op jit(solution)/shard_map/bhn,khn->bhk/dot_general | solution.py:47
  50.0 0.1 iota_compare_fusion
  50.2 2.8 %fusion.39 = (f32[32,64]{1,0:T(8,128)S(1)}, f32[32,64,128]{2,1,0:T(8,128)S(1)}) fusion(f32[32,64,128]{2,1,0:T(8,128)S(1)} %fusion.25, bf16[32,128,512]{2,1,0:T(8,128)(2,1)S(1)} %copy-done, bf16[32,64,512]{2,0,1:T(8,128)(2,1)S(1)} %convert_bitcast_fusion, pred[32,128]{1,0:T(8,128)(4,1)S(1)} %iota_compare_fusion), kind=kOutput, calls=%fused_computation.53 | convolution fusion | flops 269481984 | bytes 8400896 | tf_op jit(solution)/shard_map/bhk,bsk->bhs/dot_general | solution.py:48
  52.9 0.1 fusion.26
  53.2 1.2 fusion.6
  54.4 0.7 fusion.19
  55.2 2.9 %fusion.20 = f32[32,64,512]{2,1,0:T(8,128)S(1)} fusion(bf16[32,128,512]{2,1,0:T(8,128)(2,1)} %param.16, f32[32,64,128]{2,1,0:T(8,128)S(1)} %get-tuple-element.16, f32[32,64]{1,0:T(8,128)S(1)} %exponential_add_fusion, f32[32,64]{1,0:T(8,128)S(1)} %fusion.36), kind=kOutput, calls=%fused_computation.18 | convolution fusion | flops 269221888 | bytes 9453568 | tf_op jit(solution)/shard_map/bhs,bsk->bhk/dot_general | solution.py:59
  58.2 3.7 %fusion.3.lat_ref = bf16[64,32,512]{2,1,0:T(8,128)(2,1)} fusion(f32[32,64,512]{2,1,0:T(8,128)S(1)} %fusion.20, f32[32,512]{1,0:T(8,128)S(1)} %get-tuple-element.7, f32[64,32]{1,0:T(8,128)S(1)} %copy.28), kind=kLoop, calls=%fused_computation.4 | loop fusion | flops 3145728 | bytes 6365184 | tf_op jit(solution)/shard_map/convert_element_type | solution.py:60
  61.9 8.0 %head_values.1.o_ref = bf16[32,8192]{1,0:T(8,128)(2,1)} custom-call(bf16[64,32,512]{2,1,0:T(8,128)(2,1)} %fusion.3.lat_ref, bf16[512,8192]{1,0:T(8,128)(2,1)} %val_ref.1), custom_call_target="tpu_custom_call" | custom-call | flops 268435456 | bytes 8388608 | tf_op jit(solution)/shard_map/head_values/pallas_call | solution.py:79
  69.9 0.6 reshape.107.gain_ref
  70.6 118.6 %tail.1 = bf16[32,7168]{1,0:T(8,128)(2,1)} custom-call(bf16[32,8192]{1,0:T(8,128)(2,1)} %head_values.1.o_ref, bf16[32,7168]{1,0:T(8,128)(2,1)} %x_ref.3, bf16[1,7168]{1,0:T(2,128)(2,1)} %reshape.107.gain_ref, bf16[8192,7168]{1,0:T(8,128)(2,1)} %wo_hbm.1, bf16[7168,1152]{1,0:T(8,128)(2,1)} %wg_hbm.1, bf16[7168,1152]{1,0:T(8,128)(2,1)} %wu_hbm.1, ...), custom_call_target="tpu_custom_call" | custom-call | tf_op jit(solution)/shard_map/tail/pallas_call | solution.py:539
  189.2 1.4 pad_maximum_fusion.3
  190.5 1.8 copy.61
  (29 shorter events, 0.4 us)
Async XLA Ops:
  2.0 39.2 %copy-start.9 = (s32[32]{0:T(128)S(1)}, s32[32]{0:T(128)}, u32[]{:S(2)}) copy-start(s32[32]{0:T(128)} %param.18) | copy-start | bytes 388
  40.4 4.5 %copy-start.2 = (bf16[32,128,64]{1,2,0:T(8,128)(2,1)S(1)}, bf16[32,128,64]{1,2,0:T(8,128)(2,1)}, u32[]{:S(2)}) copy-start(bf16[32,128,64]{1,2,0:T(8,128)(2,1)} %param.17) | copy-start | bytes 1572868
  41.3 3.0 %copy-start.4 = (bf16[32,32]{1,0:T(8,128)(2,1)}, bf16[32,32]{1,0:T(8,128)(2,1)S(1)}, u32[]{:S(2)}) copy-start(bf16[32,32]{1,0:T(8,128)(2,1)S(1)} %get-tuple-element.11) | copy-start | bytes 6148
  41.4 3.0 %copy-start.5 = (bf16[32,32]{1,0:T(8,128)(2,1)}, bf16[32,32]{1,0:T(8,128)(2,1)S(1)}, u32[]{:S(2)}) copy-start(bf16[32,32]{1,0:T(8,128)(2,1)S(1)} %get-tuple-element.12) | copy-start | bytes 6148
  43.7 3.4 %copy-start.1 = (bf16[512,8192]{1,0:T(8,128)(2,1)S(1)}, bf16[512,8192]{1,0:T(8,128)(2,1)}, u32[]{:S(2)}) copy-start(bf16[512,8192]{1,0:T(8,128)(2,1)} %param.23) | copy-start | bytes 25165828
  47.0 3.1 %copy-start = (bf16[32,128,512]{2,1,0:T(8,128)(2,1)S(1)}, bf16[32,128,512]{2,1,0:T(8,128)(2,1)}, u32[]{:S(2)}) copy-start(bf16[32,128,512]{2,1,0:T(8,128)(2,1)} %param.16) | copy-start | bytes 12582916
  50.1 2.8 %copy-start.3 = (bf16[32,576]{1,0:T(8,128)(2,1)S(1)}, bf16[32,576]{1,0:T(8,128)(2,1)}, u32[]{:S(2)}) copy-start(bf16[32,576]{1,0:T(8,128)(2,1)} %get-tuple-element.6) | copy-start | bytes 110596
  50.1 2.9 %copy-start.8 = (bf16[512]{0:T(512)(128)(2,1)S(1)}, bf16[512]{0:T(512)(128)(2,1)}, u32[]{:S(2)}) copy-start(bf16[512]{0:T(512)(128)(2,1)} %param.22) | copy-start | bytes 3076
  53.2 1.9 copy-start.6
  61.9 8.0 %copy-start.7 = (bf16[7168]{0:T(1024)(128)(2,1)S(1)}, bf16[7168]{0:T(1024)(128)(2,1)}, u32[]{:S(2)}) copy-start(bf16[7168]{0:T(1024)(128)(2,1)} %param.26) | copy-start | bytes 43012

commit v4 on v2

--- a/solution.py
+++ b/solution.py
@@ -57,14 +57,54 @@
     probs = (expo / denom[..., None]).astype(jnp.bfloat16)
     prob_new = (expo_new / denom).astype(jnp.bfloat16)
     lat_sum = jnp.einsum('bhs,bsk->bhk', probs, cache_lat, preferred_element_type=jnp.float32) + prob_new.astype(jnp.float32)[..., None] * lat_new.astype(jnp.float32)[:, None, :]
-    lat_out = lat_sum.astype(jnp.bfloat16)
-    val_up = w_val_up.reshape(value_a7, heads, -1)
-    head_out = jnp.einsum('bhk,khv->bhv', lat_out, val_up, preferred_element_type=jnp.float32).astype(jnp.bfloat16).reshape(rows, -1)
+    head_out = head_values(lat_sum, w_val_up)
     return head_out, lat_new, rope_new
 
 MESH = pl.DeviceIdType.MESH
-GATHER_LAG = 2
+GATHER_LAG = 1
 SCATTER_LAG = 2
+
+def head_kernel(heads, lat_ref, val_ref, out_ref, lat_buf):
+    rows = out_ref.shape[0]
+    width = val_ref.shape[1]
+    dim = width // heads
+    lanes, total, _ = lat_buf.shape
+    quad, group = 4, 16
+    step = total // 16
+
+    @pl.loop(0, 16)
+    def _(b):
+        rs = pl.ds(pl.multiple_of(b * step, step), step)
+        for i in range(lanes):
+            lat_buf[i, rs, :] = lat_ref[rs, i * 128:(i + 1) * 128]
+
+    @pl.loop(0, heads // group)
+    def _(c):
+        for g in range(group // quad):
+            first = c * group + g * quad
+            parts = [jnp.concatenate([lat_buf[i, pl.ds(first + k, rows, stride=heads), :] for k in range(quad)], axis=0) for i in range(lanes)]
+            lhs = jnp.concatenate(parts, axis=1).astype(jnp.bfloat16)
+            cols = pl.ds(pl.multiple_of(first * dim, quad * dim), quad * dim)
+            prod = jnp.dot(lhs, val_ref[:, cols], preferred_element_type=jnp.float32)
+            diag = [prod[k * rows:(k + 1) * rows, k * dim:(k + 1) * dim] for k in range(quad)]
+            out_ref[:, cols] = jnp.concatenate(diag, axis=1).astype(jnp.bfloat16)
+
+
+def head_values(lat_sum, w_val_up):
+    rows, heads, depth = lat_sum.shape
+    width = w_val_up.shape[1]
+    vmem = pl.BlockSpec(memory_space=pltpu.VMEM)
+    return pl.pallas_call(
+        functools.partial(head_kernel, heads),
+        out_shape=jax.ShapeDtypeStruct((rows, width), jnp.bfloat16),
+        in_specs=[vmem, vmem],
+        out_specs=vmem,
+        scratch_shapes=[pltpu.VMEM((depth // 128, rows * heads, 128), jnp.float32)],
+        cost_estimate=pl.CostEstimate(flops=2 * rows * depth * width, bytes_accessed=2 * depth * width, transcendentals=0),
+        compiler_params=pltpu.CompilerParams(vmem_limit_bytes=24_000_000),
+        name='head_values',
+    )(lat_sum.reshape(rows * heads, depth), w_val_up)
+
 
 def query_kernel(sub, x_ref, gain_ref, wq_hbm, wkv_hbm, q_ref, kv_ref,
                  h_all, w_buf, wkv_buf, stage, kv_part, kv_stage, kv_in,
@@ -90,7 +130,7 @@
         slot = lax.rem(i, slots)
         return pltpu.make_async_copy(wq_hbm.at[:, pl.ds(pl.multiple_of(core * q_half + i * sub, 128), sub)], w_buf.at[slot], w_sem.at[slot])
 
-    wkv_copy = pltpu.make_async_copy(wkv_hbm.at[my_depth, :], wkv_buf, wkv_sem.at[0])
+    wkv_copy = pltpu.make_async_copy(wkv_hbm.at[:, my_depth], wkv_buf, wkv_sem.at[0])
     wkv_copy.start()
     for i in range(slots):
         w_copy(i).start()
@@ -108,7 +148,7 @@
     inv = lax.rsqrt(jnp.sum(tot, axis=1, keepdims=True) / width + EPS)
     for c in range(0, width, step):
         vals = x_ref[:, c:c + step].astype(f32)
-        h_all[my_rows, c:c + step] = (vals * inv * gain_ref[:, c:c + step].astype(f32)).astype(bf16)
+        h_all[my_rows, c:c + step] = (vals * inv * gain_ref[c:c + step].astype(f32)[None, :]).astype(bf16)
 
     pl.semaphore_wait(barrier, 1)
     h_push = remote(h_all.at[my_rows, :], h_all.at[my_rows, :], h_send.at[0], h_recv.at[0])
@@ -116,7 +156,7 @@
     remote(h_all.at[their_rows, :], h_all.at[their_rows, :], h_send.at[0], h_recv.at[0]).wait_recv()
 
     wkv_copy.wait()
-    kv_part[...] = jnp.dot(h_all[:, my_depth], wkv_buf[...], preferred_element_type=f32)
+    kv_part[...] = lax.dot_general(h_all[:, my_depth], wkv_buf[...], (((1,), (1,)), ((), ())), preferred_element_type=f32)
     kv_stage[...] = kv_part[their_rows, :]
     kv_push = remote(kv_stage, kv_in, k_send.at[0], k_recv.at[0])
     kv_push.start()
@@ -166,7 +206,7 @@
     scratch = [
         pltpu.VMEM((2 * rows, width), bf16),
         pltpu.VMEM((slots, width, sub), bf16),
-        pltpu.VMEM((width // 2, kv_cols), bf16),
+        pltpu.VMEM((kv_cols, width // 2), bf16),
         pltpu.VMEM((tiles, rows, sub), bf16),
         pltpu.VMEM((2 * rows, kv_cols), f32),
         pltpu.VMEM((rows, kv_cols), f32),
@@ -181,7 +221,7 @@
         scratch_shapes=scratch,
         compiler_params=pltpu.CompilerParams(collective_id=1, has_side_effects=True, vmem_limit_bytes=60_000_000),
         name='query',
-    )(hidden, attn_norm.reshape(1, width), w_query, w_kv_down)
+    )(hidden, attn_norm, w_query, w_kv_down.T)
 
 
 def tail_kernel(n, tile, sub, o_ref, x_ref, gain_ref, wo_hbm, wg_hbm, wu_hbm, wd_hbm, out_ref,
@@ -250,7 +290,7 @@
     x_push.start()
     o_all[my_rows, :] = o_ref[...]
     x_half[my_rows, :] = x_ref[:, pl.ds(mine, half)]
-    gain = gain_ref[...].astype(f32)
+    gain = gain_ref[...].astype(f32)[None, :]
     gain_top = jnp.maximum(jnp.max(jnp.abs(gain), axis=1, keepdims=True), 1e-30)
     gain_s[...] = gain / gain_top
     acc[...] = jnp.zeros_like(acc)
@@ -479,7 +519,7 @@
                     sum_copy(t, h, d).wait_send()
 
 
-def fused_tail(n, head_out, hidden, mlp_norm, w_out, w_gate, w_up, w_down, tile=256, sub=256):
+def fused_tail(n, head_out, hidden, mlp_norm, w_out, w_gate, w_up, w_down, tile=512, sub=256):
     bf16, f32 = jnp.bfloat16, jnp.float32
     rows, width = hidden.shape
     inner = head_out.shape[1]
@@ -523,7 +563,7 @@
         scratch_shapes=scratch,
         compiler_params=pltpu.CompilerParams(collective_id=0, has_side_effects=True, vmem_limit_bytes=67_043_328),
         name='tail',
-    )(head_out, hidden, mlp_norm.reshape(1, width), w_out, w_gate, w_up, w_down)
+    )(head_out, hidden, mlp_norm, w_out, w_gate, w_up, w_down)
 
 
 def solution(mesh):

time: 208 us -> 186 us (0.89)
  local copies, waits for them, and re-layouts: 20.5 us -> 6.86 us
  matrix products: 18.7 us -> 9.37 us
  other arithmetic: 4.03 us -> 6.79 us
    unnamed x24 -> x15, local copies, waits for them, and re-layouts: 15.9 us -> 4.42 us
    dot_general x1 -> x0, matrix products: 8.21 us -> none  [attention_block(): jnp.einsum('bhk,khv->bhv', lat_out, val_up, preferred_element_type=jnp.fl...]
    pallas_call x1, Pallas kernels: 126 us -> 119 us  [fused_tail(): pl.pallas_call(functools.partial(tail_kernel, n, tile, sub), out_shape=ja...]
    pallas_call x0 -> x1, Pallas kernels: none -> 5.1 us  [head_values(): pl.pallas_call(functools.partial(head_kernel, heads), out_shape=jax.Shape...]
    reshape x3 -> x0, local copies, waits for them, and re-layouts: 2.15 us -> none  [the longest x1 0.9 us: attention_block(): jnp.einsum('bhk,khv->bhv', lat_out, val_up, preferred_element_type=jnp.fl...]
where the time goes in v4:
time: 186 us
  Pallas kernels  162 us (87%)
  matrix products  9.37 us (5%)
  local copies, waits for them, and re-layouts  6.86 us (4%)
  other arithmetic  6.79 us (4%)
    pallas_call x1, Pallas kernels, fused_tail(): pl.pallas_call(functools.partial(tail_kernel, n, tile, sub), out_shape=ja...  119 us
    pallas_call x1, Pallas kernels, paired_query(): pl.pallas_call(functools.partial(query_kernel, sub), out_shape=(jax.Shape...  38.4 us
    pallas_call x1, Pallas kernels, head_values(): pl.pallas_call(functools.partial(head_kernel, heads), out_shape=jax.Shape...  5.1 us
    unnamed x15, local copies, waits for them, and re-layouts  4.42 us

profile of v4, /device:TPU:21, one launch (start us, length us, event | category | flops | bytes accessed | tf_op | source)
XLA Modules:
  0.0 185.9 jit_solution(7908921235431631144)
XLA Ops:
  0.6 0.7 convert_element_type.41
  1.3 0.7 convert_element_type.43
  2.0 0.7 iota_compare_fusion
  2.7 38.4 %query.1 = (bf16[32,12288]{1,0:T(8,128)(2,1)}, bf16[32,576]{1,0:T(8,128)(2,1)}) custom-call(bf16[32,7168]{1,0:T(8,128)(2,1)} %x_ref.3, bf16[7168]{0:T(1024)(128)(2,1)} %gain_ref.2, bf16[7168,12288]{1,0:T(8,128)(2,1)} %wq_hbm.1, bf16[576,7168]{1,0:T(8,128)(2,1)} %bitcast.26), custom_call_target="tpu_custom_call" | custom-call | tf_op jit(solution)/shard_map/query/pallas_call | solution.py:216
  41.1 0.9 fusion.24
  42.0 0.7 slice_convert_fusion.1
  42.7 0.1 subtract_convert_fusion.1
  43.0 0.7 pad_maximum_fusion.3
  43.6 0.8 fusion.34
  44.5 2.3 %reshape.101 = bf16[32,64,192]{2,1,0:T(8,128)(2,1)S(1)} reshape(bf16[32,12288]{1,0:T(8,128)(2,1)} %get-tuple-element.5) | data formatting | bytes 1572864 | tf_op jit(solution)/shard_map/reshape | solution.py:41
  47.0 0.1 slice_convert_fusion
  47.1 0.6 subtract_convert_fusion
  47.7 0.4 fusion.22
  48.1 0.4 fusion.23
  48.5 1.8 copy-done.2
  50.3 3.0 %convert_bitcast_fusion = bf16[32,64,512]{2,0,1:T(8,128)(2,1)S(1)} fusion(bf16[32,64,128]{2,1,0:T(8,128)(2,1)S(1)} %slice.32, bf16[512,8192]{1,0:T(8,128)(2,1)S(1)} %copy-done.2), kind=kOutput, calls=%fused_computation.4 | convolution fusion | flops 269484032 | bytes 11010048 | tf_op jit(solution)/shard_map/bhn,khn->bhk/dot_general | solution.py:47
  53.3 2.8 %fusion.36 = (f32[32,64]{1,0:T(8,128)S(1)}, f32[32,64,128]{2,1,0:T(8,128)S(1)}) fusion(f32[32,64,128]{2,1,0:T(8,128)S(1)} %fusion.23, bf16[32,128,512]{2,1,0:T(8,128)(2,1)S(1)} %copy-done.1, bf16[32,64,512]{2,0,1:T(8,128)(2,1)S(1)} %convert_bitcast_fusion, pred[32,128]{1,0:T(8,128)(4,1)S(1)} %iota_compare_fusion), kind=kOutput, calls=%fused_computation.49 | convolution fusion | flops 269481984 | bytes 8400896 | tf_op jit(solution)/shard_map/bhk,bsk->bhs/dot_general | solution.py:48
  56.1 1.2 fusion.5
  57.3 0.7 fusion.18
  58.0 1.5 multiply_add_fusion
  59.6 5.1 %head_values.1.o_ref = bf16[32,8192]{1,0:T(8,128)(2,1)S(1)} custom-call(f32[2048,512]{1,0:T(8,128)S(1)} %bitcast.23, bf16[512,8192]{1,0:T(8,128)(2,1)S(1)} %bitcast.25), custom_call_target="tpu_custom_call" | custom-call | flops 268435456 | bytes 8388608 | tf_op jit(solution)/shard_map/head_values/pallas_call | solution.py:97
  64.7 0.8 copy-done
  65.5 118.6 %tail.1 = bf16[32,7168]{1,0:T(8,128)(2,1)} custom-call(bf16[32,8192]{1,0:T(8,128)(2,1)} %copy-done, bf16[32,7168]{1,0:T(8,128)(2,1)} %x_ref.3, bf16[7168]{0:T(1024)(128)(2,1)} %gain_ref.3, bf16[8192,7168]{1,0:T(8,128)(2,1)} %wo_hbm.1, bf16[7168,1152]{1,0:T(8,128)(2,1)} %wg_hbm.1, bf16[7168,1152]{1,0:T(8,128)(2,1)} %wu_hbm.1, bf16[1152,7168]{1,0:T(8,128)(2,1)} %wd_hbm.1), custom_call_target="tpu_custom_call" | custom-call | tf_op jit(solution)/shard_map/tail/pallas_call | solution.py:558
  184.1 1.8 copy.52
  (19 shorter events, 0.3 us)
Async XLA Ops:
  44.5 11.6 %copy-start.4 = (bf16[32,512]{1,0:T(8,128)(2,1)}, bf16[32,512]{1,0:T(8,128)(2,1)S(1)}, u32[]{:S(2)}) copy-start(bf16[32,512]{1,0:T(8,128)(2,1)S(1)} %get-tuple-element.23) | copy-start | bytes 98308
  44.5 3.6 %copy-start.3 = (bf16[32,128,64]{1,2,0:T(8,128)(2,1)S(1)}, bf16[32,128,64]{1,2,0:T(8,128)(2,1)}, u32[]{:S(2)}) copy-start(bf16[32,128,64]{1,2,0:T(8,128)(2,1)} %param.17) | copy-start | bytes 1572868
  46.9 3.4 %copy-start.2 = (bf16[512,8192]{1,0:T(8,128)(2,1)S(1)}, bf16[512,8192]{1,0:T(8,128)(2,1)}, u32[]{:S(2)}) copy-start(bf16[512,8192]{1,0:T(8,128)(2,1)} %param.23) | copy-start | bytes 25165828
  50.3 3.0 %copy-start.1 = (bf16[32,128,512]{2,1,0:T(8,128)(2,1)S(1)}, bf16[32,128,512]{2,1,0:T(8,128)(2,1)}, u32[]{:S(2)}) copy-start(bf16[32,128,512]{2,1,0:T(8,128)(2,1)} %param.16) | copy-start | bytes 12582916
  53.3 6.3 %slice-start = ((s8[8388608]{0:T(1024)(128)(4,1)}), s8[4194304]{0:T(1024)(128)(4,1)S(1)}, s32[]{:S(2)}) async-start(s8[8388608]{0:T(1024)(128)(4,1)} %bitcast.24), calls=%async_computation | async-start | bytes 8388608
  56.1 3.5 %slice-start.1 = ((s8[8388608]{0:T(1024)(128)(4,1)}), s8[4194304]{0:T(1024)(128)(4,1)S(1)}, s32[]{:S(2)}) async-start(s8[8388608]{0:T(1024)(128)(4,1)} %bitcast.24), calls=%async_computation.1 | async-start | bytes 8388608
  64.7 0.8 copy-start

commit v5 on v4

--- a/solution.py
+++ b/solution.py
@@ -371,17 +371,21 @@
         @pl.when(j < tiles)
         def _():
             produce(j)
-        for h in range(1, reach_max + 1):
-            t = j - GATHER_LAG * h
-
-            @pl.when((t >= 0) & (t < tiles))
-            def _():
-                forward(t, h)
+        def forward_hops(hops):
+            for h in hops:
+                t = j - GATHER_LAG * h
+
+                @pl.when((t >= 0) & (t < tiles))
+                def _():
+                    forward(t, h)
+
         t_use = j - last_hop - 1
+        forward_hops(range(1, 2))
 
         @pl.when((t_use >= 0) & (t_use < tiles))
         def _():
             consume(t_use)
+        forward_hops(range(2, reach_max + 1))
         t_next = j - last_hop + 1
 
         @pl.when((t_next >= 0) & (t_next < tiles))

time: 186 us -> 189 us (1.016)
  Pallas kernels: 162 us -> 165 us
    pallas_call x1, Pallas kernels: 119 us -> 121 us  [fused_tail(): pl.pallas_call(functools.partial(tail_kernel, n, tile, sub), out_shape=ja...]
where the time goes in v5:
time: 189 us
  Pallas kernels  165 us (87%)
  matrix products  9.37 us (5%)
  local copies, waits for them, and re-layouts  6.86 us (4%)
  other arithmetic  6.79 us (4%)
    pallas_call x1, Pallas kernels, fused_tail(): pl.pallas_call(functools.partial(tail_kernel, n, tile, sub), out_shape=ja...  121 us
    pallas_call x1, Pallas kernels, paired_query(): pl.pallas_call(functools.partial(query_kernel, sub), out_shape=(jax.Shape...  38.4 us
    pallas_call x1, Pallas kernels, head_values(): pl.pallas_call(functools.partial(head_kernel, heads), out_shape=jax.Shape...  5.1 us
    unnamed x15, local copies, waits for them, and re-layouts  4.42 us

profile of v5, /device:TPU:21, one launch (start us, length us, event | category | flops | bytes accessed | tf_op | source)
XLA Modules:
  0.0 188.6 jit_solution(7508609796719866350)
XLA Ops:
  0.6 0.7 convert_element_type.41
  1.3 0.7 convert_element_type.43
  2.0 0.7 iota_compare_fusion
  2.7 38.4 %query.1 = (bf16[32,12288]{1,0:T(8,128)(2,1)}, bf16[32,576]{1,0:T(8,128)(2,1)}) custom-call(bf16[32,7168]{1,0:T(8,128)(2,1)} %x_ref.3, bf16[7168]{0:T(1024)(128)(2,1)} %gain_ref.2, bf16[7168,12288]{1,0:T(8,128)(2,1)} %wq_hbm.1, bf16[576,7168]{1,0:T(8,128)(2,1)} %bitcast.26), custom_call_target="tpu_custom_call" | custom-call | tf_op jit(solution)/shard_map/query/pallas_call | solution.py:216
  41.1 0.9 fusion.24
  42.0 0.7 slice_convert_fusion.1
  42.7 0.1 subtract_convert_fusion.1
  43.0 0.7 pad_maximum_fusion.3
  43.6 0.8 fusion.34
  44.5 2.3 %reshape.101 = bf16[32,64,192]{2,1,0:T(8,128)(2,1)S(1)} reshape(bf16[32,12288]{1,0:T(8,128)(2,1)} %get-tuple-element.5) | data formatting | bytes 1572864 | tf_op jit(solution)/shard_map/reshape | solution.py:41
  47.0 0.1 slice_convert_fusion
  47.1 0.6 subtract_convert_fusion
  47.7 0.4 fusion.22
  48.1 0.4 fusion.23
  48.5 1.8 copy-done.2
  50.3 3.0 %convert_bitcast_fusion = bf16[32,64,512]{2,0,1:T(8,128)(2,1)S(1)} fusion(bf16[32,64,128]{2,1,0:T(8,128)(2,1)S(1)} %slice.32, bf16[512,8192]{1,0:T(8,128)(2,1)S(1)} %copy-done.2), kind=kOutput, calls=%fused_computation.4 | convolution fusion | flops 269484032 | bytes 11010048 | tf_op jit(solution)/shard_map/bhn,khn->bhk/dot_general | solution.py:47
  53.3 2.8 %fusion.36 = (f32[32,64]{1,0:T(8,128)S(1)}, f32[32,64,128]{2,1,0:T(8,128)S(1)}) fusion(f32[32,64,128]{2,1,0:T(8,128)S(1)} %fusion.23, bf16[32,128,512]{2,1,0:T(8,128)(2,1)S(1)} %copy-done.1, bf16[32,64,512]{2,0,1:T(8,128)(2,1)S(1)} %convert_bitcast_fusion, pred[32,128]{1,0:T(8,128)(4,1)S(1)} %iota_compare_fusion), kind=kOutput, calls=%fused_computation.49 | convolution fusion | flops 269481984 | bytes 8400896 | tf_op jit(solution)/shard_map/bhk,bsk->bhs/dot_general | solution.py:48
  56.1 1.2 fusion.5
  57.3 0.7 fusion.18
  58.0 1.5 multiply_add_fusion
  59.6 5.1 %head_values.1.o_ref = bf16[32,8192]{1,0:T(8,128)(2,1)S(1)} custom-call(f32[2048,512]{1,0:T(8,128)S(1)} %bitcast.23, bf16[512,8192]{1,0:T(8,128)(2,1)S(1)} %bitcast.25), custom_call_target="tpu_custom_call" | custom-call | flops 268435456 | bytes 8388608 | tf_op jit(solution)/shard_map/head_values/pallas_call | solution.py:97
  64.7 0.8 copy-done
  65.5 121.2 %tail.1 = bf16[32,7168]{1,0:T(8,128)(2,1)} custom-call(bf16[32,8192]{1,0:T(8,128)(2,1)} %copy-done, bf16[32,7168]{1,0:T(8,128)(2,1)} %x_ref.3, bf16[7168]{0:T(1024)(128)(2,1)} %gain_ref.3, bf16[8192,7168]{1,0:T(8,128)(2,1)} %wo_hbm.1, bf16[7168,1152]{1,0:T(8,128)(2,1)} %wg_hbm.1, bf16[7168,1152]{1,0:T(8,128)(2,1)} %wu_hbm.1, bf16[1152,7168]{1,0:T(8,128)(2,1)} %wd_hbm.1), custom_call_target="tpu_custom_call" | custom-call | tf_op jit(solution)/shard_map/tail/pallas_call | solution.py:562
  186.7 1.8 copy.52
  (19 shorter events, 0.3 us)
Async XLA Ops:
  44.5 11.6 %copy-start.4 = (bf16[32,512]{1,0:T(8,128)(2,1)}, bf16[32,512]{1,0:T(8,128)(2,1)S(1)}, u32[]{:S(2)}) copy-start(bf16[32,512]{1,0:T(8,128)(2,1)S(1)} %get-tuple-element.23) | copy-start | bytes 98308
  44.5 3.6 %copy-start.3 = (bf16[32,128,64]{1,2,0:T(8,128)(2,1)S(1)}, bf16[32,128,64]{1,2,0:T(8,128)(2,1)}, u32[]{:S(2)}) copy-start(bf16[32,128,64]{1,2,0:T(8,128)(2,1)} %param.17) | copy-start | bytes 1572868
  46.9 3.4 %copy-start.2 = (bf16[512,8192]{1,0:T(8,128)(2,1)S(1)}, bf16[512,8192]{1,0:T(8,128)(2,1)}, u32[]{:S(2)}) copy-start(bf16[512,8192]{1,0:T(8,128)(2,1)} %param.23) | copy-start | bytes 25165828
  50.3 3.0 %copy-start.1 = (bf16[32,128,512]{2,1,0:T(8,128)(2,1)S(1)}, bf16[32,128,512]{2,1,0:T(8,128)(2,1)}, u32[]{:S(2)}) copy-start(bf16[32,128,512]{2,1,0:T(8,128)(2,1)} %param.16) | copy-start | bytes 12582916
  53.3 6.3 %slice-start = ((s8[8388608]{0:T(1024)(128)(4,1)}), s8[4194304]{0:T(1024)(128)(4,1)S(1)}, s32[]{:S(2)}) async-start(s8[8388608]{0:T(1024)(128)(4,1)} %bitcast.24), calls=%async_computation | async-start | bytes 8388608
  56.1 3.5 %slice-start.1 = ((s8[8388608]{0:T(1024)(128)(4,1)}), s8[4194304]{0:T(1024)(128)(4,1)S(1)}, s32[]{:S(2)}) async-start(s8[8388608]{0:T(1024)(128)(4,1)} %bitcast.24), calls=%async_computation.1 | async-start | bytes 8388608
  64.7 0.8 copy-start
